TPU v7x, 32 devices: a whole 2x2x4 slice. The times are simulated.
32 devices in a mesh: gz: 16 (over z, x, core), gy: 2 (over y).
Axes of the slice: x: 2, y: 2, z: 4, core: 2. Of those that a mesh axis runs over, the one named last changes fastest.
Arguments:
- spread_weights: float32 [64, 32768], P(None, ('gz', 'gy')), may hold values from -6 to 6
- spread_base: int32 [3, 32768], P(None, ('gz', 'gy')), may hold values from 0 to 383, as said below
- qm_base: int32 [3, 4096], P(None, ('gz', 'gy')), may hold values from 0 to 383, as said below
- qm_frac: float32 [3, 4096], P(None, ('gz', 'gy')), may hold values from 0 to 1
- qm_charge: float32 [4096], P(('gz', 'gy')), may hold values from -3 to 3
Outputs:
- qm_forces: float32 [3, 4096], P(None, ('gz', 'gy'))
Inputs may be any that keep to these rules, and one draw needn't show every extreme that they name: For point charge j let d = j // 1024, p = d // 2 and q = d % 2; then spread_base[0, j] lies in [p * 24, (p + 1) * 24) and spread_base[1, j] in [q * 192, (q + 1) * 192); spread_base[2, j] is any cell. For quantum-region atom i let d = i // 128, p = d // 2 and q = d % 2; then qm_base[0, i] lies in [p * 24, (p + 1) * 24) and qm_base[1, i] in [q * 192, (q + 1) * 192); qm_base[2, i] is any cell.
All inputs are finite; a program needn't handle non-finite values.
Results may differ from a plain program's by a relative error of at most 0.0003.
Values sent between devices are 32-bit elements; how exact they have to be, the bound alone decides.
A program may use at most 256 MiB of HBM per device.

v0:
```python
import math

import jax
import jax.numpy as jnp
from jax import lax
from jax.experimental import pallas as pl
from jax.experimental.pallas import tpu as pltpu
from jax.sharding import PartitionSpec as P

GRID = 384
ORDER = 4


SPLITTING = 0.8
HIGHEST = lax.Precision.HIGHEST
HIGH = lax.Precision.HIGH
GROUP = 64


def moduli(index, points):
    signed = jnp.where(index < points // 2, index, index - points).astype(jnp.float32) / points
    spline = 2.0 / 3.0 + jnp.cos(2.0 * math.pi / points * index.astype(jnp.float32)) / 3.0
    return (signed * signed, 1.0 / (spline * spline), index == points // 2)


def influence(first, second, third, points):
    sq_one, mod_one, edge_one = moduli(first, points)
    sq_two, mod_two, edge_two = moduli(second, points)
    sq_three, mod_three, edge_three = moduli(third, points)
    total = sq_one + sq_two + sq_three
    safe = jnp.where(total > 0.0, total, 1.0)
    value = (
        mod_one
        * mod_two
        * mod_three
        * jnp.exp(-(math.pi * math.pi / (SPLITTING * SPLITTING)) * total)
        / (math.pi * safe)
    )
    keep = (total > 0.0) & jnp.logical_not(edge_one | edge_two | edge_three)
    return jnp.where(keep, value, 0.0)


def spline_weights(frac):
    remain = 1.0 - frac
    square = frac * frac
    cubed = square * frac
    values = jnp.stack(
        [
            remain * remain * remain / 6.0,
            (3.0 * cubed - 6.0 * square + 4.0) / 6.0,
            (-3.0 * cubed + 3.0 * square + 3.0 * frac + 1.0) / 6.0,
            cubed / 6.0,
        ]
    )
    slopes = jnp.stack(
        [
            -0.5 * remain * remain,
            (3.0 * square - 4.0 * frac) / 2.0,
            (-3.0 * square + 2.0 * frac + 1.0) / 2.0,
            0.5 * square,
        ]
    )
    return (values, slopes)


def angle_tables(rows_in, cols_in, points):
    product = rows_in[:, None] * cols_in[None, :] % points
    angle = 2.0 * math.pi / points * product.astype(jnp.float32)
    return (jnp.cos(angle), jnp.sin(angle))


def line_tables(cells, values, slopes, extent):
    hits = (jnp.arange(extent, dtype=jnp.int32)[None, :, None] == cells[:, None, :]).astype(
        jnp.float32
    )
    return (jnp.sum(hits * values[:, None, :], axis=0), jnp.sum(hits * slopes[:, None, :], axis=0))


def spread_kernel(first_ref, count_ref, weights_ref, z_ref, y_ref, waves_ref, out_ref):
    half = pl.program_id(0)
    group = pl.program_id(1)

    @pl.when(group == 0)
    def _():
        out_ref[...] = jnp.zeros_like(out_ref)

    rows = out_ref.shape[1]
    weights = weights_ref[...]
    z_cell = z_ref[...]
    y_cell = y_ref[...]
    waves = waves_ref[...]
    high = waves.astype(jnp.bfloat16)
    low = (waves - high.astype(jnp.float32)).astype(jnp.bfloat16)
    first = first_ref[half, group]
    row_offset = lax.broadcasted_iota(jnp.int32, (rows, weights.shape[1]), 0) - y_cell

    def plane(step, carry):
        z = first + step
        offset = z - z_cell
        chosen = jnp.zeros((ORDER, weights.shape[1]), jnp.float32)
        for a in range(ORDER):
            chosen = jnp.where(offset == a, weights[a * ORDER : (a + 1) * ORDER], chosen)
        placed = jnp.zeros((rows, weights.shape[1]), jnp.float32)
        for b in range(ORDER):
            placed = jnp.where(row_offset == b, chosen[b : b + 1], placed)
        top = placed.astype(jnp.bfloat16)
        rest = (placed - top.astype(jnp.float32)).astype(jnp.bfloat16)
        total = jnp.dot(top, high, preferred_element_type=jnp.float32)
        total += jnp.dot(rest, high, preferred_element_type=jnp.float32)
        total += jnp.dot(top, low, preferred_element_type=jnp.float32)
        out_ref[z] += total
        return carry

    lax.fori_loop(0, count_ref[half, group], plane, 0)


def sort_by_plane(table, local_z):
    count = local_z.shape[0]
    order = jnp.arange(count, dtype=jnp.int32)
    before = (local_z[:, None] < local_z[None, :]) | (
        (local_z[:, None] == local_z[None, :]) & (order[:, None] < order[None, :])
    )
    rank = jnp.sum(before.astype(jnp.int32), axis=0)
    moves = (rank[:, None] == order[None, :]).astype(jnp.float32)
    return jnp.dot(table, moves, precision=HIGHEST)


def phases(cells, index, points):
    angle = (2.0 * math.pi / points) * (cells[..., None] * index % points).astype(jnp.float32)
    return (jnp.cos(angle), jnp.sin(angle))


def spread_lines(spread_weights, spread_base, z_first, y_first, z_extent, y_local, kx_index, points):
    count = spread_weights.shape[1]
    halves = lax.axis_size("gy")
    local = jnp.stack([spread_base[0] - z_first, spread_base[1] - y_first, spread_base[2]])
    table = jnp.concatenate([spread_weights, local.astype(jnp.float32)], axis=0)
    table = sort_by_plane(table, local[0])
    table = lax.all_gather(table, "gy")
    groups = count // GROUP
    width = ORDER * GROUP
    weights = table[:, : ORDER**3].reshape(halves, ORDER * ORDER, ORDER, groups, GROUP)
    weights = weights.transpose(0, 3, 1, 2, 4).reshape(halves, groups, ORDER * ORDER, width)
    cells = jnp.round(table[:, ORDER**3 :]).astype(jnp.int32).reshape(halves, 3, groups, GROUP)
    z_cell, y_cell, x_cell = cells[:, 0], cells[:, 1], cells[:, 2]
    first = jnp.min(z_cell, axis=-1)
    planes = jnp.max(z_cell, axis=-1) - first + ORDER
    z_wide = jnp.tile(z_cell, (1, 1, ORDER))[:, :, None, :]
    y_wide = jnp.tile(y_cell, (1, 1, ORDER))[:, :, None, :]
    cosine, sine = phases(x_cell, kx_index, points)
    step_cos, step_sin = phases(jnp.arange(ORDER, dtype=jnp.int32), kx_index, points)
    step_cos, step_sin = step_cos[:, None, :], step_sin[:, None, :]
    cosine, sine = cosine[:, :, None], sine[:, :, None]
    waves = jnp.concatenate(
        [cosine * step_cos - sine * step_sin, -(sine * step_cos + cosine * step_sin)], axis=-1
    ).reshape(halves, groups, width, -1)
    rows = -(-(y_local + ORDER - 1) // 8) * 8
    lanes = waves.shape[-1]
    per_group = lambda q, g, *_: (q, g, 0, 0)
    lines = pl.pallas_call(
        spread_kernel,
        grid_spec=pltpu.PrefetchScalarGridSpec(
            num_scalar_prefetch=2,
            grid=(halves, groups),
            in_specs=[
                pl.BlockSpec((None, None, ORDER * ORDER, width), per_group),
                pl.BlockSpec((None, None, 1, width), per_group),
                pl.BlockSpec((None, None, 1, width), per_group),
                pl.BlockSpec((None, None, width, lanes), per_group),
            ],
            out_specs=pl.BlockSpec((z_extent, None, rows, lanes), lambda q, g, *_: (0, q, 0, 0)),
        ),
        out_shape=jax.ShapeDtypeStruct((z_extent, halves, rows, lanes), jnp.float32),
        compiler_params=pltpu.CompilerParams(dimension_semantics=("arbitrary", "arbitrary")),
    )(first, planes, weights, z_wide, y_wide, waves)
    return lines, rows


def line_waves(cell, values, slopes, index, points):
    cosine, sine = phases(cell, index, points)
    step_cos, step_sin = phases(jnp.arange(ORDER, dtype=jnp.int32), index, points)
    found = []
    for table in (values, slopes):
        real = sum(table[c][..., None] * step_cos[c] for c in range(ORDER))
        imag = sum(table[c][..., None] * step_sin[c] for c in range(ORDER))
        found.append((cosine * real - sine * imag, cosine * imag + sine * real))
    return found


def slab_forces(lines, base, frac, z_first, y_index, x_index, points):
    z_extent, ky_local, _, kx_local = lines.shape
    shifts = jnp.arange(ORDER, dtype=jnp.int32)[:, None]
    w_z, d_z = spline_weights(frac[0])
    w_y, d_y = spline_weights(frac[1])
    w_x, d_x = spline_weights(frac[2])
    plane_w, plane_d = line_tables(base[0][None, :] - z_first + shifts, w_z, d_z, z_extent)
    (wy_re, wy_im), (dy_re, dy_im) = line_waves(base[1], w_y, d_y, y_index, points)
    (wx_re, wx_im), (dx_re, dx_im) = line_waves(base[2], w_x, d_x, x_index, points)
    join = lambda a, b: jnp.concatenate([a, b], axis=1)
    waves = jnp.stack([join(wx_re, -wx_im), join(wx_im, wx_re), join(dx_re, -dx_im), join(dx_im, dx_re)])
    count = base.shape[1]
    along = jnp.einsum(
        "mk,nk->mn",
        lines.reshape(z_extent * ky_local, 2 * kx_local),
        waves.reshape(4 * count, 2 * kx_local),
        precision=HIGH,
    ).reshape(z_extent, ky_local, 4, count)
    wy_re, wy_im, dy_re, dy_im = wy_re.T, wy_im.T, dy_re.T, dy_im.T
    plain = jnp.sum(along[:, :, 0] * wy_re - along[:, :, 1] * wy_im, axis=1)
    tilted = jnp.sum(along[:, :, 0] * dy_re - along[:, :, 1] * dy_im, axis=1)
    sloped = jnp.sum(along[:, :, 2] * wy_re - along[:, :, 3] * wy_im, axis=1)
    return jnp.stack(
        [
            jnp.sum(plain * plane_d, axis=0),
            jnp.sum(tilted * plane_w, axis=0),
            jnp.sum(sloped * plane_w, axis=0),
        ]
    )


def shards(spread_weights, spread_base, qm_base, qm_frac, qm_charge):
    points = GRID
    margin = ORDER - 1
    count_z = lax.axis_size("gz")
    count_y = lax.axis_size("gy")
    z_local = points // count_z
    y_local = points // count_y
    z_extent = z_local + margin
    kx_count = points // 2
    kx_local = kx_count // count_y
    ky_local = points // count_z
    z_first = lax.axis_index("gz") * z_local
    y_first = lax.axis_index("gy") * y_local
    ky_index = lax.axis_index("gz") * ky_local + jnp.arange(ky_local, dtype=jnp.int32)
    kx_index = lax.axis_index("gy") * kx_local + jnp.arange(kx_local, dtype=jnp.int32)
    positions = jnp.arange(points, dtype=jnp.int32)
    all_base = lax.all_gather(qm_base, ("gz", "gy"), axis=1, tiled=True)
    all_frac = lax.all_gather(qm_frac, ("gz", "gy"), axis=1, tiled=True)

    lines, rows = spread_lines(
        spread_weights, spread_base, z_first, y_first, z_extent, y_local, kx_index, points
    )
    row_cells = (
        jnp.arange(count_y, dtype=jnp.int32)[:, None] * y_local
        + jnp.arange(rows, dtype=jnp.int32)[None, :]
    ).reshape(-1) % points
    tables = jnp.concatenate(angle_tables(positions, row_cells, points), axis=0)
    lines = lines.reshape(z_extent, count_y * rows, 2 * kx_local)
    both = jnp.einsum("yr,zrk->zyk", tables, lines, precision=HIGH)
    with_cos, with_sin = both[:, :points], both[:, points:]
    packed = jnp.stack(
        [
            with_cos[:, :, :kx_local] + with_sin[:, :, kx_local:],
            with_cos[:, :, kx_local:] - with_sin[:, :, :kx_local],
        ],
        axis=1,
    )
    packed = packed.reshape(z_extent, 2, count_z, ky_local, kx_local).transpose(2, 0, 1, 3, 4)
    packed = packed.reshape(count_z, z_extent * 2 * ky_local * kx_local)
    moved = lax.all_to_all(packed, "gz", split_axis=0, concat_axis=0, tiled=True)

    z_cells = (
        jnp.arange(count_z, dtype=jnp.int32)[:, None] * z_local
        + jnp.arange(z_extent, dtype=jnp.int32)[None, :]
    ).reshape(-1) % points
    cells = ky_local * kx_local
    moved = moved.reshape(count_z * z_extent, 2 * cells)
    tables = jnp.concatenate(angle_tables(positions, z_cells, points), axis=0)
    both = jnp.dot(tables, moved, precision=HIGH).reshape(2, points, 2, ky_local, kx_local)
    green = influence(
        positions[:, None, None], ky_index[None, :, None], kx_index[None, None, :], points
    )
    kx_weight = jnp.where(kx_index == 0, 1.0, 2.0).astype(jnp.float32)
    green = green * (kx_weight * (1.0 / float(points * points * points)))
    spectrum = jnp.stack(
        [(both[0, :, 0] + both[1, :, 1]) * green, (both[0, :, 1] - both[1, :, 0]) * green], axis=1
    ).reshape(points, 2 * cells)
    back = jnp.concatenate(angle_tables(z_cells, positions, points), axis=0)
    both = jnp.dot(back, spectrum, precision=HIGH)
    both = both.reshape(2, count_z, z_extent, 2, ky_local, kx_local)
    lines = jnp.stack(
        [both[0, :, :, 0] - both[1, :, :, 1], both[0, :, :, 1] + both[1, :, :, 0]], axis=3
    )

    def one_slab(args):
        slab, base, frac, start = args
        return slab_forces(slab, base, frac, start, ky_index, kx_index, points)

    slab_base = all_base.reshape(3, count_z, -1).transpose(1, 0, 2)
    slab_frac = all_frac.reshape(3, count_z, -1).transpose(1, 0, 2)
    starts = jnp.arange(count_z, dtype=jnp.int32) * z_local
    partial = lax.map(one_slab, (lines, slab_base, slab_frac, starts))
    forces = lax.psum_scatter(
        partial.transpose(1, 0, 2).reshape(3, -1), ("gz", "gy"), scatter_dimension=1, tiled=True
    )
    return -qm_charge * forces


def solution(mesh):
    in_specs = (
        P(None, ("gz", "gy")),
        P(None, ("gz", "gy")),
        P(None, ("gz", "gy")),
        P(None, ("gz", "gy")),
        P(("gz", "gy")),
    )
    out_specs = P(None, ("gz", "gy"))
    return jax.shard_map(shards, mesh=mesh, in_specs=in_specs, out_specs=out_specs, check_vma=False)
```

profile of v0, /device:TPU:0, one launch (start us, length us, event | category | flops | bytes accessed | tf_op | source)
XLA Modules:
  0.0 874.4 jit_solution(13381775178883817362)
XLA Ops:
  10.8 10.7 %all-gather.1 = f32[2,67,1024]{2,1,0:T(8,128)S(1)} all-gather(f32[1,67,1024]{2,1,0:T(8,128)S(1)} %fusion.84), channel_id=2, replica_groups=mesh['gz'=16,'gy'=2] {'gy'}, dimensions={0}, use_global_device_ids=true | all-gather | bytes 823296 | tf_op jit(solution)/shard_map/all_gather | solution.py:139
  21.9 5.7 fusion.90
  36.5 5.5 pad_maximum_fusion.3.waves_ref
  42.5 55.5 %shard_map.55 = f32[27,2,200,192]{3,2,1,0:T(8,128)} custom-call(s32[2,16]{1,0:T(2,128)} %copy-done.1, s32[2,16]{1,0:T(2,128)} %subtract_add_fusion.count_ref, f32[2,16,16,256]{3,2,1,0:T(8,128)} %reshape.2142.weights_ref, s32[2,16,1,256]{3,2,1,0:T(1,128)} %tile.20.z_ref, s32[2,16,1,256]{3,2,1,0:T(1,128)} %tile.23.y_ref, ...), custom_call_target="tpu_custom_call" | custom-call | tf_op jit(solution)/shard_map/pallas_call | solution.py:160
  98.0 21.7 %convolution_bitcast_fusion = f32[27,768,192]{1,2,0:T(8,128)} fusion(f32[27,400,192]{2,1,0:T(8,128)} %bitcast.230, f32[384,400]{0,1:T(8,128)S(1)} %get-tuple-element.286, f32[384,400]{0,1:T(8,128)S(1)} %get-tuple-element.285), kind=kOutput, calls=%fused_computation.150 | convolution fusion | flops 9555456000 | bytes 25448448 | tf_op jit(solution)/shard_map/yr,zrk->zyk/dot_general | solution.py:249
  119.7 10.1 %slice_add_fusion.1 = (f32[27,384,96]{1,2,0:T(8,128)}, f32[27,384,96]{1,2,0:T(8,128)}) fusion(f32[27,768,192]{1,2,0:T(8,128)} %convolution_bitcast_fusion), kind=kLoop, calls=%fused_computation.179 | loop fusion | flops 1990656 | bytes 23887872 | tf_op jit(solution)/shard_map/add | solution.py:253
  129.8 5.9 copy.52
  135.7 5.9 copy.53
  146.5 4.9 copy.54
  151.4 17.5 %all_to_all.8 = f32[16,1,124416]{2,1,0:T(1,128)} reshape(f32[16,27,2,24,96]{4,3,2,1,0:T(8,128)} %copy.54) | data formatting | bytes 15925248 | tf_op jit(solution)/shard_map/all_to_all | solution.py:260
  168.9 6.5 all-to-all-start
  183.3 184.2 %all_gather.14 = s32[3,4096]{1,0:T(4,128)S(1)} all-gather(s32[3,128]{1,0:T(4,128)S(1)} %copy-done.2), channel_id=1, replica_groups=mesh['gz'=16,'gy'=2] {'gz','gy'}, dimensions={1}, use_global_device_ids=true | all-gather | bytes 50688 | tf_op jit(solution)/shard_map/all_gather | solution.py:237
  367.5 91.7 %all_gather.15 = f32[3,4096]{1,0:T(4,128)S(1)} all-gather(f32[3,128]{1,0:T(4,128)S(1)} %copy-done.3), channel_id=1, replica_groups=mesh['gz'=16,'gy'=2] {'gz','gy'}, dimensions={1}, use_global_device_ids=true | all-gather | bytes 50688 | tf_op jit(solution)/shard_map/all_gather | solution.py:238
  459.7 71.6 %reduce.2 = f32[16,124416]{1,0:T(8,128)} reduce(f32[16,1,124416]{2,1,0:T(1,128)} %all-to-all-done, f32[]{:T(128)} %constant.275), dimensions={1}, to_apply=%all_to_all.7.reduce_sub_computation | reduce | bytes 15925252 | tf_op jit(solution)/shard_map/all_to_all | solution.py:260
  531.3 6.3 reshape.2144
  537.6 9.3 %copy.56 = f32[4608,432]{1,0:T(8,128)} copy(f32[4608,432]{0,1:T(8,128)} %bitcast.232) | data formatting | bytes 15925248 | tf_op jit(solution)/shard_map/dot_general | solution.py:269
  546.9 14.7 %fusion.80 = f32[2,384,2,24,96]{1,4,3,2,0:T(8,128)S(1)} fusion(f32[2,24,96,432,1]{3,2,1,0,4:T(8,128)} %bitcast.231, f32[2,384,432,1,1]{1,0,2,4,3:T(2,128)S(1)} %bitcast.236), kind=kOutput, calls=%fused_computation.198 | convolution fusion | flops 9172942848 | bytes 23445504 | tf_op jit(solution)/shard_map/dot_general | solution.py:269
  564.7 23.1 %fusion.55 = f32[2,16,27,2,24,96]{5,2,4,3,1,0:T(8,128)} fusion(f32[384,1,24,96]{0,3,2,1:T(8,128)S(1)} %get-tuple-element.268, f32[384,1,24,96]{0,3,2,1:T(8,128)S(1)} %get-tuple-element.267, f32[2,16,27,384,1,1]{3,2,1,0,4,5:T(8,128)S(1)} %reshape.2158), kind=kOutput, calls=%fused_computation.153 | convolution fusion | flops 9174712320 | bytes 24330240 | tf_op jit(solution)/shard_map/dot_general | solution.py:279
  587.8 6.2 fusion.58
  594.0 9.1 %fusion.60 = f32[16,27,24,1,96]{4,1,2,0,3:T(8,128)} fusion(f32[2,16,27,2,24,96]{5,2,4,3,1,0:T(8,128)} %fusion.55), kind=kLoop, calls=%fused_computation.163 | loop fusion | flops 995328 | bytes 11943936 | tf_op jit(solution)/shard_map/sub | solution.py:282
  603.1 9.4 %pad_maximum_fusion.2 = f32[16,27,24,2,96]{4,1,2,0,3:T(8,128)} fusion(f32[16,27,24,1,96]{4,1,2,0,3:T(8,128)S(1)} %fusion.58, f32[16,27,24,1,96]{4,1,2,0,3:T(8,128)} %fusion.60), kind=kLoop, calls=%fused_computation.148 | loop fusion | flops 1990656 | bytes 15925248 | tf_op jit(solution)/shard_map/stack | solution.py:281
  612.5 20.0 %copy.60 = f32[16,27,24,2,96]{4,3,2,1,0:T(2,128)} copy(f32[16,27,24,2,96]{4,1,2,0,3:T(8,128)} %pad_maximum_fusion.2) | data formatting | bytes 15925248
  632.5 96.8 %while.13 = (s32[]{:T(128)}, f32[16,3,256]{2,1,0:T(4,128)S(1)}, f32[16,27,24,2,96]{4,3,2,1,0:T(2,128)}, s32[16,3,256]{2,1,0:T(4,128)S(1)}, f32[16,3,256]{2,1,0:T...) while((s32[]{:T(128)}, f32[16,3,256]{2,1,0:T(4,128)S(1)}, ...), condition=%wide.region_12.13_spmd.clone, body=%wide.region_3.12_spmd.clone.sunk | while | flops 768924544 | bytes 11141737 | solution.py:292
  731.4 134.2 %reduce-scatter.4.cloned.1.call-done = f32[128,3]{1,0:T(8,128)} async-done(((f32[4096,3]{1,0:T(8,128)}), f32[128,3]{1,0:T(8,128)}) %reduce-scatter.4.cloned.1.call-update) | async-done | bytes 1552
  (500 shorter events, 128.1 us)
Async XLA Ops:
  21.9 20.1 %copy-start.1 = (s32[2,16]{1,0:T(2,128)}, s32[2,16]{1,0:T(2,128)S(1)}, u32[]{:S(2)}) copy-start(s32[2,16]{1,0:T(2,128)S(1)} %get-tuple-element.274.first_ref) | copy-start | bytes 388
  168.9 290.8 %all-to-all-start = ((f32[16,1,124416]{2,1,0:T(1,128)}), f32[16,1,124416]{2,1,0:T(1,128)}, u32[]{:S(2)}, u32[]{:S(2)}) async-start(f32[16,1,124416]{2,1,0:T(1,128)} %all_to_all.8), calls=%async_computation | async-start | bytes 15925248 | tf_op jit(solution)/shard_map/all_to_all | solution.py:260
  175.4 690.3 %reduce-scatter.4.cloned.1.call-start = ((), (), s32[]{:S(2)}) async-start(), calls=%async_computation.2 | async-start | bytes 2162688
  178.5 4.8 copy-start.2
  178.5 189.1 %copy-start.3 = (f32[3,128]{1,0:T(4,128)S(1)}, f32[3,128]{1,0:T(4,128)}, u32[]{:S(2)}) copy-start(f32[3,128]{1,0:T(4,128)} %param.10) | copy-start | bytes 4612
  537.6 9.3 %copy-start = (f32[2,384,432]{1,0,2:T(2,128)S(1)}, f32[2,384,432]{1,0,2:T(2,128)}, u32[]{:S(2)}) copy-start(f32[2,384,432]{1,0,2:T(2,128)} %dot_general.30) | copy-start | bytes 3981316
  729.4 2.0 copy-start.4
Sparse Core Ops, SparseCore 0:
  731.5 134.0 reduce-scatter.3
where the time goes:
time: 884 us; the launch traced here: 874 us
  blocking collectives  287 us (32%)
  other arithmetic  179 us (20%)
  waiting for transfers between devices  134 us (15%)
  local copies, waits for them, and re-layouts  113 us (13%)
  matrix products  82.2 us (9%)
  Pallas kernels  55.5 us (6%)
  between operations  14.2 us (2%)
    all_gather x1, blocking collectives, shards(): all_base = lax.all_gather(qm_base, ('gz', 'gy'), axis=1, tiled=True)  184 us
    unnamed x2, waiting for transfers between devices  134 us
    all_gather x1, blocking collectives, shards(): all_frac = lax.all_gather(qm_frac, ('gz', 'gy'), axis=1, tiled=True)  91.7 us
    all_to_all x1, other arithmetic, shards(): lax.all_to_all(packed, 'gz', split_axis=0, concat_axis=0, tiled=True)  71.6 us
    pallas_call x1, Pallas kernels, spread_lines(): pl.pallas_call(spread_kernel, grid_spec=pltpu.PrefetchScalarGridSpec(num_...  55.5 us
    dynamic_slice x32, local copies, waits for them, and re-layouts, shards(): partial = lax.map(one_slab, (lines, slab_base, slab_frac, starts))  28 us
    dot_general x1, matrix products, shards(): both = jnp.dot(back, spectrum, precision=HIGH)  23.1 us
    unnamed x13, local copies, waits for them, and re-layouts  22.9 us
  transfers between devices with their start and end apart: 2, of which 1 were waited for; matrix products, arithmetic and copies ran while one was open for 1% of the time, Pallas kernels for 0%

commit v1 on v0

--- a/solution.py
+++ b/solution.py
@@ -1,7 +1,9 @@
+import functools
 import math
 
 import jax
 import jax.numpy as jnp
+import numpy as np
 from jax import lax
 from jax.experimental import pallas as pl
 from jax.experimental.pallas import tpu as pltpu
@@ -296,6 +298,609 @@
     return -qm_charge * forces
 
 
+MESH = pl.DeviceIdType.MESH
+RING = 4
+PLANE = 4
+LANES = 128
+F32 = jnp.float32
+BF16 = jnp.bfloat16
+VMEM_LIMIT = 62 * 2**20
+
+
+def split_table(table):
+    high = table.astype(np.float32).astype(BF16)
+    low = (table - high.astype(np.float64)).astype(np.float32).astype(BF16)
+    return jnp.asarray(high), jnp.asarray(low)
+
+
+def split(value):
+    high = value.astype(BF16)
+    return high, (value - high.astype(F32)).astype(BF16)
+
+
+def dot3(a_high, a_low, b_high, b_low):
+    total = jnp.dot(a_high, b_high, preferred_element_type=F32)
+    total += jnp.dot(a_low, b_high, preferred_element_type=F32)
+    return total + jnp.dot(a_high, b_low, preferred_element_type=F32)
+
+
+def trig(units, points):
+    rest = units - points * jnp.floor((units + 0.5) * (1.0 / points))
+    quarter = points // 4
+    turn = jnp.floor((rest + quarter / 2) * (1.0 / quarter))
+    angle = (rest - quarter * turn) * (2.0 * math.pi / points)
+    square = angle * angle
+    sine = angle * (1.0 + square * (-1.0 / 6 + square * (1.0 / 120 + square * (-1.0 / 5040 + square / 362880))))
+    cosine = 1.0 + square * (-0.5 + square * (1.0 / 24 + square * (-1.0 / 720 + square * (1.0 / 40320))))
+    odd = (turn == 1.0) | (turn == 3.0)
+    first = jnp.where(odd, sine, cosine)
+    second = jnp.where(odd, cosine, sine)
+    first = jnp.where((turn == 1.0) | (turn == 2.0), -first, first)
+    second = jnp.where((turn == 2.0) | (turn == 3.0), -second, second)
+    return first, second
+
+
+def wave_units(lane, kx_first, kx_local):
+    sine = lane >= kx_local
+    index = jnp.where(sine, lane - kx_local, lane)
+    index = jnp.where(index >= kx_local, 0, index)
+    return (kx_first + index).astype(F32), sine
+
+
+def order_by(key, table):
+    count = key.shape[0]
+    order = jnp.arange(count, dtype=jnp.int32)
+    before = (key[:, None] < key[None, :]) | ((key[:, None] == key[None, :]) & (order[:, None] < order[None, :]))
+    rank = jnp.sum(before.astype(jnp.int32), axis=0)
+    moves = (rank[:, None] == order[None, :]).astype(F32)
+    return jnp.dot(table, moves, precision=HIGHEST)
+
+
+def gather_kernel(count_z, count_y, own_ref, halo_ref, qm_ref, tab_ref, all_ref, own_send, own_recv, halo_send, halo_recv, qm_send, qm_recv):
+    p = lax.axis_index("gz")
+    y = lax.axis_index("gy")
+    me = p * count_y + y
+    total = count_z * count_y
+    barrier = pltpu.get_barrier_semaphore()
+    for d in range(1, total):
+        other = lax.rem(me + d, total)
+        pl.semaphore_signal(barrier, inc=1, device_id=(other // count_y, lax.rem(other, count_y)), device_id_type=MESH)
+    pl.semaphore_wait(barrier, total - 1)
+    copies = []
+
+    def send(src, dst, s, r, device):
+        copy = pltpu.make_async_remote_copy(src_ref=src, dst_ref=dst, send_sem=s, recv_sem=r, device_id=device, device_id_type=MESH)
+        copy.start()
+        copies.append(copy)
+
+    upper = lax.rem(p + 1, count_z)
+    send(own_ref, tab_ref.at[y, 0], own_send, own_recv, (p, 1 - y))
+    send(halo_ref, tab_ref.at[y, 1], halo_send.at[0], halo_recv.at[0], (upper, y))
+    send(halo_ref, tab_ref.at[y, 1], halo_send.at[1], halo_recv.at[1], (upper, 1 - y))
+    whole = len(copies)
+    for d in range(1, total):
+        other = lax.rem(me + d, total)
+        send(qm_ref, all_ref.at[me], qm_send, qm_recv, (other // count_y, lax.rem(other, count_y)))
+    tab_ref[y, 0] = own_ref[...]
+    all_ref[me] = qm_ref[...]
+    for copy in copies[:whole]:
+        copy.wait()
+    rest = pltpu.make_async_remote_copy(
+        src_ref=all_ref.at[pl.ds(0, total - 1)], dst_ref=all_ref.at[pl.ds(0, total - 1)],
+        send_sem=qm_send, recv_sem=qm_recv, device_id=(p, 1 - y), device_id_type=MESH)
+    rest.wait()
+
+
+def gather(own, halo, qm, count_z, count_y):
+    vmem = pl.BlockSpec(memory_space=pltpu.VMEM)
+    dma = pltpu.SemaphoreType.DMA
+    return pl.pallas_call(
+        functools.partial(gather_kernel, count_z, count_y),
+        out_shape=(
+            jax.ShapeDtypeStruct((count_y, 2) + own.shape, F32),
+            jax.ShapeDtypeStruct((count_z * count_y,) + qm.shape, F32),
+        ),
+        in_specs=[vmem] * 3,
+        out_specs=(vmem, vmem),
+        scratch_shapes=[dma, dma, dma((2,)), dma((2,)), dma, dma],
+        compiler_params=pltpu.CompilerParams(collective_id=0, has_side_effects=True, vmem_limit_bytes=VMEM_LIMIT),
+        name="gather_atoms",
+    )(own, halo, qm)
+
+
+def lines_kernel(points, kx_local, kx_ref, first_ref, count_ref, tab_ref, out_ref, placed_ref, high_ref, low_ref):
+    half, seg, block = pl.program_id(0), pl.program_id(1), pl.program_id(2)
+    blocks = pl.num_programs(2)
+
+    @pl.when((seg == 0) & (block == 0))
+    def _():
+        out_ref[...] = jnp.zeros_like(out_ref)
+
+    lane = lax.broadcasted_iota(jnp.int32, (1, LANES), 1)
+    wide = lax.broadcasted_iota(jnp.int32, (1, 2 * LANES), 1)
+    kx, sine = wave_units(wide, kx_ref[0], kx_local)
+    shift = jnp.where(sine, points - points // 4, points).astype(F32)
+    z_rows = out_ref.shape[2]
+    part = LANES // 2
+
+    def group(h, steps, z_used):
+        index = ((half * 2 + seg) * blocks + block) * 2 + h
+
+        @pl.when(count_ref[index] > 0)
+        def _():
+            tab = tab_ref[...]
+
+            def pair(even, odd):
+                if h == 0:
+                    return jnp.where(lane < part, even, pltpu.roll(odd, part, 1))
+                return jnp.where(lane < part, pltpu.roll(even, part, 1), odd)
+
+            rows = ORDER * ORDER
+            weights = jnp.concatenate(
+                [pair(tab[0:rows], tab[rows : 2 * rows]), pair(tab[2 * rows : 3 * rows], tab[3 * rows : 4 * rows])], axis=1)
+            spots = tab[4 * rows : 4 * rows + 8]
+            spots_pair = pair(spots, spots)
+            spots_wide = jnp.concatenate([spots_pair, spots_pair], axis=1).astype(jnp.int32)
+            z_off = lax.broadcasted_iota(jnp.int32, (z_used, 2 * LANES), 0) - spots_wide[0:1]
+            y_cell = spots_wide[1:2]
+            for b in range(ORDER):
+                chosen = jnp.zeros((z_used, 2 * LANES), F32)
+                for a in range(ORDER):
+                    chosen = jnp.where(z_off == a, weights[a * ORDER + b : a * ORDER + b + 1], chosen)
+                placed_ref[b, 0:z_used] = chosen
+            column = jnp.broadcast_to(spots[2:3], (LANES, LANES)).T[h * part : (h + 1) * part]
+            column = jnp.concatenate([column, column], axis=1)
+            cosine, sinus = trig(kx * column + shift, points)
+            step = lax.broadcasted_iota(jnp.int32, (8, 2 * LANES), 0).astype(F32)
+            step_cos, step_sin = trig(kx * step, points)
+            for c in range(ORDER):
+                wave = cosine * step_cos[c : c + 1] - sinus * step_sin[c : c + 1] if c else cosine
+                high, low = split(wave)
+                high_ref[c * part : (c + 1) * part] = high
+                low_ref[c * part : (c + 1) * part] = low
+            first = first_ref[index]
+
+            def rows_of(it, carry):
+                y_first = first + it * steps
+                pieces = []
+                for s in range(steps):
+                    off = (y_first + s) - y_cell
+                    placed = jnp.zeros((z_used, 2 * LANES), F32)
+                    for b in range(ORDER):
+                        placed = jnp.where(off == b, placed_ref[b, 0:z_used], placed)
+                    pieces.append(placed)
+                top, rest = split(jnp.concatenate(pieces, axis=0))
+                total = dot3(top, rest, high_ref[...], low_ref[...])
+                for t in range(2):
+                    part_of = total[:, t * LANES : (t + 1) * LANES].reshape(steps, z_used, LANES)
+                    out_ref[t, pl.ds(y_first, steps), 0:z_used, :] += part_of
+                return carry
+
+            lax.fori_loop(0, count_ref[index], rows_of, 0)
+
+    for h in range(2):
+
+        @pl.when(seg == 0)
+        def _():
+            group(h, OWN_STEP, z_rows)
+
+        @pl.when(seg == 1)
+        def _():
+            group(h, HALO_STEP, 8)
+
+
+OWN_STEP = 16
+HALO_STEP = 32
+
+
+def spread(tab, kx_first, kx_local, z_local, y_local, points):
+    halves, segs, rows, count = tab.shape
+    extent = -(-(y_local + ORDER - 1 + HALO_STEP - 1) // 8) * 8
+    part = LANES // 2
+    cells = jnp.round(tab[:, :, 4 * ORDER * ORDER : 4 * ORDER * ORDER + 2]).astype(jnp.int32)
+    cells = cells.reshape(halves, segs, 2, count // part, part)
+    z_cell, y_cell = cells[:, :, 0], cells[:, :, 1]
+    live = z_cell > -ORDER
+    low = jnp.min(jnp.where(live, y_cell, points), axis=-1)
+    top = jnp.max(jnp.where(live, y_cell, -points), axis=-1) + ORDER
+    steps = jnp.asarray([OWN_STEP, HALO_STEP], jnp.int32)[None, :, None]
+    counts = jnp.maximum((top - low + steps - 1) // steps, 0)
+    return pl.pallas_call(
+        functools.partial(lines_kernel, points, kx_local),
+        grid_spec=pltpu.PrefetchScalarGridSpec(
+            num_scalar_prefetch=3,
+            grid=(halves, segs, count // LANES),
+            in_specs=[pl.BlockSpec((None, None, rows, LANES), lambda h, s, b, *_: (h, s, 0, b))],
+            out_specs=pl.BlockSpec((2, None, extent, z_local, LANES), lambda h, s, b, *_: (0, h, 0, 0, 0)),
+            scratch_shapes=[
+                pltpu.VMEM((ORDER, z_local, 2 * LANES), F32),
+                pltpu.VMEM((2 * LANES, 2 * LANES), BF16),
+                pltpu.VMEM((2 * LANES, 2 * LANES), BF16),
+            ],
+        ),
+        out_shape=jax.ShapeDtypeStruct((2, halves, extent, z_local, LANES), F32),
+        compiler_params=pltpu.CompilerParams(
+            dimension_semantics=("arbitrary",) * 3, vmem_limit_bytes=VMEM_LIMIT),
+        name="spread_lines",
+    )(kx_first.reshape(1), low.reshape(-1), counts.reshape(-1), tab)
+
+
+def flip_of(a, b):
+    ax, ac = a // 2, lax.rem(a, 2)
+    bx, bc = b // 2, b % 2
+    return 2 * jnp.abs(ax - bx) + jnp.abs(ac - bc)
+
+
+def rows_kernel(z_local, groups, here_ref, lines_ref, high_ref, low_ref, out_ref):
+    ring, spot = here_ref[0], here_ref[1]
+    lane = lax.broadcasted_iota(jnp.int32, (8, LANES), 1)
+    deep = lines_ref.shape[1] // z_local
+    packed_rows = 12 * groups
+
+    def plane(z, carry):
+        data = jnp.concatenate(
+            [lines_ref[t, pl.ds(z, deep, stride=z_local), :] for t in range(2)], axis=1)
+        high, low = split(data)
+        out = dot3(high_ref[...], low_ref[...], high, low)
+        for p in range(RING * PLANE):
+            slot = lax.rem(p // PLANE - ring + RING, RING) * PLANE + flip_of(spot, p % PLANE)
+            for g in range(groups):
+                rows = out[(g * RING * PLANE + p) * 8 :][:8]
+                base = (slot * packed_rows + g * 12) * z_local + z
+                out_ref[pl.ds(base, 8, stride=z_local), :] = rows[:, :LANES]
+                tail = rows[:, LANES:]
+                tail = jnp.where(lane < LANES // 2, tail, pltpu.roll(pltpu.roll(tail, LANES // 2, 1), 4, 0))
+                out_ref[pl.ds(base + 8 * z_local, 4, stride=z_local), :] = tail[:4]
+        return carry
+
+    lax.fori_loop(0, z_local, plane, 0)
+
+
+def transform_rows(lines, here, y_local, points):
+    tiles, halves, extent, z_local, width = lines.shape
+    parts = RING * PLANE
+    block = points // parts
+    groups = block // 8
+    g, p, r = np.meshgrid(np.arange(groups), np.arange(parts), np.arange(8), indexing="ij")
+    ky = ((p // 2) * block + g * 8 + r).reshape(-1)
+    sine = (p % 2).reshape(-1)
+    cell = (np.arange(halves)[:, None] * y_local + np.arange(extent)[None, :]).reshape(-1) % points
+    angle = 2.0 * np.pi / points * ((ky[:, None] * cell[None, :]) % points)
+    table = np.where(sine[:, None] == 0, np.cos(angle), np.sin(angle))
+    high, low = split_table(table)
+    vmem = pl.BlockSpec(memory_space=pltpu.VMEM)
+    out = pl.pallas_call(
+        functools.partial(rows_kernel, z_local, groups),
+        in_specs=[pl.BlockSpec(memory_space=pltpu.SMEM), vmem, vmem, vmem],
+        out_specs=vmem,
+        out_shape=jax.ShapeDtypeStruct((parts * 12 * groups * z_local, LANES), F32),
+        compiler_params=pltpu.CompilerParams(vmem_limit_bytes=VMEM_LIMIT),
+        name="transform_rows",
+    )(here, lines.reshape(tiles, halves * extent * z_local, width), high, low)
+    return out.reshape(RING, PLANE, 12 * groups, z_local, LANES)
+
+
+CHUNKS = 6
+
+
+def exchange_kernel(send_ref, out_ref, cross_ref, relay_ref, s_near, r_near, s_cross, r_cross, s_hop, r_hop, s_relay, r_relay, s_last, r_last):
+    p = lax.axis_index("gz")
+    y = lax.axis_index("gy")
+    ring, spot = p // PLANE, lax.rem(p, PLANE)
+    x, core = spot // 2, lax.rem(spot, 2)
+    spots = [spot, x * 2 + 1 - core, (1 - x) * 2 + core, (1 - x) * 2 + 1 - core]
+    up, down = lax.rem(ring + 1, RING), lax.rem(ring + RING - 1, RING)
+    above, below = up * PLANE + spot, down * PLANE + spot
+    across = [ring * PLANE + s for s in spots]
+    rows = send_ref.shape[2] // CHUNKS
+    z_local = send_ref.shape[3]
+    barrier = pltpu.get_barrier_semaphore()
+    for other in across[1:] + [above, below]:
+        pl.semaphore_signal(barrier, inc=1, device_id=(other, y), device_id_type=MESH)
+    pl.semaphore_wait(barrier, PLANE + 1)
+
+    def copy(src, dst, s, r, device):
+        return pltpu.make_async_remote_copy(src_ref=src, dst_ref=dst, send_sem=s, recv_sem=r, device_id=(device, y), device_id_type=MESH)
+
+    def span(j):
+        return pl.ds(j * rows, rows)
+
+    def held(d, z, j):
+        return send_ref.at[z, 0, span(j)] if d == 0 else cross_ref.at[d - 1, z - 1, span(j)]
+
+    for j in range(CHUNKS):
+        for d in (2, 3, 1):
+            copy(send_ref.at[pl.ds(1, RING - 1), d, span(j)], cross_ref.at[d - 1, :, span(j)], s_cross.at[j], r_cross.at[j], across[d]).start()
+    for j in range(CHUNKS):
+        for d in (2, 3, 1):
+            copy(send_ref.at[0, d, span(j)], out_ref.at[span(j), p], s_near.at[j], r_near.at[j], across[d]).start()
+    for i in range(out_ref.shape[0]):
+        out_ref[i, p] = send_ref[0, 0, i]
+    big = lambda j: cross_ref.at[:, :, span(j)]
+    three = lambda j: cross_ref.at[0, :, span(j)]
+    four = lambda j: relay_ref.at[:, span(j)]
+    eight = lambda j: send_ref.at[pl.ds(0, 2), :, span(j)]
+
+    def hop(j):
+        copy(big(j), big(j), s_cross.at[j], r_cross.at[j], above).wait_recv()
+        for d in (0, 1, 2, 3):
+            copy(held(d, 2, j), relay_ref.at[d, span(j)], s_relay.at[j], r_relay.at[j], above if d < 2 else below).start()
+        for d in (0, 1, 2, 3):
+            copy(held(d, 1, j), out_ref.at[span(j), across[d]], s_hop.at[j], r_hop.at[j], above).start()
+            copy(held(d, 3, j), out_ref.at[span(j), across[d]], s_hop.at[j], r_hop.at[j], below).start()
+
+    def forward(j):
+        copy(four(j), four(j), s_relay.at[j], r_relay.at[j], above).wait_recv()
+        for d in (0, 1, 2, 3):
+            origin = (down if d < 2 else up) * PLANE + spots[d]
+            copy(relay_ref.at[d, span(j)], out_ref.at[span(j), origin], s_last.at[j], r_last.at[j], above if d < 2 else below).start()
+
+    def finish(j):
+        copy(three(j), three(j), s_near.at[j], r_near.at[j], above).wait_recv()
+        copy(eight(j), eight(j), s_hop.at[j], r_hop.at[j], above).wait_recv()
+        copy(four(j), four(j), s_last.at[j], r_last.at[j], above).wait_recv()
+
+    for j in range(CHUNKS):
+        hop(j)
+        if j >= 1:
+            forward(j - 1)
+    forward(CHUNKS - 1)
+    for j in range(CHUNKS):
+        finish(j)
+    for j in range(CHUNKS):
+        copy(big(j), big(j), s_cross.at[j], r_cross.at[j], above).wait_send()
+        copy(three(j), three(j), s_near.at[j], r_near.at[j], above).wait_send()
+        copy(four(j), four(j), s_relay.at[j], r_relay.at[j], above).wait_send()
+        copy(eight(j), eight(j), s_hop.at[j], r_hop.at[j], above).wait_send()
+        copy(four(j), four(j), s_last.at[j], r_last.at[j], above).wait_send()
+
+
+def exchange(send):
+    ring, plane, rows, z_local, lanes = send.shape
+    vmem = pl.BlockSpec(memory_space=pltpu.VMEM)
+    return pl.pallas_call(
+        exchange_kernel,
+        in_specs=[vmem],
+        out_specs=vmem,
+        out_shape=jax.ShapeDtypeStruct((rows, ring * plane, z_local, lanes), F32),
+        scratch_shapes=[
+            pltpu.VMEM((plane - 1, ring - 1, rows, z_local, lanes), F32),
+            pltpu.VMEM((plane, rows, z_local, lanes), F32),
+        ] + [pltpu.SemaphoreType.DMA((CHUNKS,))] * 10,
+        compiler_params=pltpu.CompilerParams(collective_id=1, has_side_effects=True, vmem_limit_bytes=VMEM_LIMIT),
+        name="exchange_blocks",
+    )(send)
+
+
+def solve_kernel(points, kx_local, block, here_ref, x_ref, fh_ref, fl_ref, bh_ref, bl_ref, az_ref, sz_ref, col_ref, sq_ref, step_ref, qm_ref, out_ref, pot_ref, wave_h, wave_l, wy_ref, acc_ref):
+    rows = x_ref.shape[0]
+    modes = points // 2
+    slabs = qm_ref.shape[0]
+    z_local = points // slabs
+    atoms = qm_ref.shape[2]
+    kx_first, ky_first, y_shift = here_ref[0], here_ref[1], here_ref[2]
+
+    def convolve(t, carry):
+        pairs = [x_ref[2 * t], x_ref[2 * t + 1]]
+        high, low = split(jnp.concatenate(pairs, axis=1))
+        coef = dot3(fh_ref[...], fl_ref[...], high, low)
+        greens = []
+        for i in range(2):
+            total = sz_ref[...] + sq_ref[pl.ds(2 * t + i, 1), :]
+            keep = total > 0.0
+            value = az_ref[...] * col_ref[pl.ds(2 * t + i, 1), :] / jnp.where(keep, total, 1.0)
+            greens.append(jnp.where(keep, value, 0.0))
+        green = jnp.concatenate(greens, axis=1)
+        high, low = split(coef * jnp.concatenate([green, green], axis=0))
+        back = dot3(bh_ref[...], bl_ref[...], high, low)
+        pot_ref[2 * t] = back[:, :LANES]
+        pot_ref[2 * t + 1] = back[:, LANES:]
+        return carry
+
+    lax.fori_loop(0, rows // 2, convolve, 0)
+    span = 4 * 8
+    wave_rows = 2 * kx_local
+    wave_h[wave_rows:] = jnp.zeros((2 * LANES - wave_rows, 2 * atoms), BF16)
+    wave_l[wave_rows:] = jnp.zeros((2 * LANES - wave_rows, 2 * atoms), BF16)
+    kx, sine = wave_units(lax.broadcasted_iota(jnp.int32, (wave_rows, atoms), 0), kx_first, kx_local)
+    x_shift = jnp.where(sine, points - points // 4, points).astype(F32)
+    ky = (ky_first + lax.broadcasted_iota(jnp.int32, (block, atoms), 0)).astype(F32)
+
+    def slab(p, carry):
+        qm = qm_ref[p]
+        row = lambda i: qm[i : i + 1]
+        cosine, sinus = trig(kx * row(2) + x_shift, points)
+        for k, at in ((0, 19), (1, 23)):
+            real = imag = None
+            for c in range(ORDER):
+                sc = jnp.concatenate([step_ref[c, 0:wave_rows]] * (atoms // LANES), axis=1)
+                ss = jnp.concatenate([step_ref[ORDER + c, 0:wave_rows]] * (atoms // LANES), axis=1)
+                real = row(at + c) * sc if real is None else real + row(at + c) * sc
+                imag = row(at + c) * ss if imag is None else imag + row(at + c) * ss
+            high, low = split(cosine * real - sinus * imag)
+            wave_h[0:wave_rows, k * atoms : (k + 1) * atoms] = high
+            wave_l[0:wave_rows, k * atoms : (k + 1) * atoms] = low
+        plain_y = slope_y = jnp.zeros((block, atoms), F32)
+        for c in range(ORDER):
+            wave, _ = trig(ky * (row(1) + float(c)) + y_shift.astype(F32), points)
+            plain_y += row(11 + c) * wave
+            slope_y += row(15 + c) * wave
+        wy_ref[0] = plain_y
+        wy_ref[1] = slope_y
+        z_first = pl.multiple_of(p * z_local, 8)
+        acc_ref[...] = jnp.zeros_like(acc_ref)
+        for g in range(block // 8):
+            tiles = []
+            for i in range(8):
+                lead = pot_ref[g * 12 + i, pl.ds(z_first, span), :]
+                tail = pot_ref[g * 12 + 8 + i % 4, pl.ds(z_first, span), :]
+                if i >= 4:
+                    tail = pltpu.roll(tail, LANES // 2, 1)
+                tiles.append(jnp.concatenate([lead, tail], axis=1))
+            high, low = split(jnp.concatenate(tiles, axis=0))
+            along = dot3(high, low, wave_h[...], wave_l[...])
+            for i in range(8):
+                r = g * 8 + i
+                value, slope = along[i * span : (i + 1) * span, :atoms], along[i * span : (i + 1) * span, atoms:]
+                wy, dy = wy_ref[0, r : r + 1], wy_ref[1, r : r + 1]
+                acc_ref[0] += value * wy
+                acc_ref[1] += value * dy
+                acc_ref[2] += slope * wy
+        off = lax.broadcasted_iota(jnp.int32, (span, atoms), 0) + z_first - row(0).astype(jnp.int32)
+        wz = dz = jnp.zeros((span, atoms), F32)
+        for a in range(ORDER):
+            wz = jnp.where(off == a, row(3 + a), wz)
+            dz = jnp.where(off == a, row(7 + a), dz)
+        total = lambda v: jnp.sum(v, axis=0, keepdims=True)
+        out_ref[p] = jnp.concatenate(
+            [total(acc_ref[0] * dz), total(acc_ref[1] * wz), total(acc_ref[2] * wz), jnp.zeros((5, atoms), F32)], axis=0)
+        return carry
+
+    lax.fori_loop(0, slabs, slab, 0)
+
+
+def solve(moved, here, qm_table, kx_index, ky_index, points):
+    rows, parts, z_local, lanes = moved.shape
+    kx_local, block = kx_index.shape[0], ky_index.shape[0]
+    half = points // 2
+    atoms = qm_table.shape[2]
+    k = np.arange(half)
+    z = np.arange(points)
+    angle = 2.0 * np.pi / points * ((k[:, None] * z[None, :]) % points)
+    forward = np.concatenate([np.cos(angle), np.sin(angle)], axis=0)
+    reach = points + 8
+    backward = forward.T[np.arange(reach) % points]
+    fh, fl = split_table(forward)
+    bh, bl = split_table(backward)
+
+    def parts_of(index):
+        square, spline, _ = moduli(index, points)
+        decay = jnp.exp(-(math.pi * math.pi / (SPLITTING * SPLITTING)) * square)
+        return square, spline * decay * jnp.where(index == 0, 1.0, 2.0)
+
+    z_sq, z_fac = parts_of(jnp.asarray(k, jnp.int32))
+    x_sq, x_fac = parts_of(kx_index)
+    y_sq, y_fac = parts_of(ky_index)
+
+    def packed(y_part, x_part, combine):
+        x_part = jnp.concatenate([x_part, x_part])
+        full = combine(y_part[:, None], x_part[None, :]).reshape(block // 8, 8, 2 * kx_local)
+        tail = full[:, :, lanes:].reshape(block // 8, 2, 4, lanes // 2).transpose(0, 2, 1, 3).reshape(block // 8, 4, lanes)
+        return jnp.concatenate([full[:, :, :lanes], tail], axis=1).reshape(rows, lanes)
+
+    col = packed(y_fac, x_fac, lambda a, b: a * b) * (1.0 / (math.pi * float(points) ** 3))
+    sq = packed(y_sq, x_sq, lambda a, b: a + b)
+    az = jnp.broadcast_to(z_fac[:, None], (half, lanes))
+    sz = jnp.broadcast_to(z_sq[:, None], (half, lanes))
+    kx_lane = jnp.concatenate([kx_index, kx_index, jnp.zeros((2 * LANES - 2 * kx_local,), jnp.int32)])
+    turn = 2.0 * math.pi / points * (jnp.arange(ORDER, dtype=jnp.int32)[:, None] * kx_lane[None, :] % points).astype(F32)
+    step = jnp.concatenate([jnp.cos(turn), jnp.sin(turn)], axis=0)
+    step = jnp.broadcast_to(step[:, :, None], step.shape + (lanes,))
+    vmem = pl.BlockSpec(memory_space=pltpu.VMEM)
+    return pl.pallas_call(
+        functools.partial(solve_kernel, points, kx_local, block),
+        in_specs=[pl.BlockSpec(memory_space=pltpu.SMEM)] + [vmem] * 11,
+        out_specs=vmem,
+        out_shape=jax.ShapeDtypeStruct((qm_table.shape[0], 8, atoms), F32),
+        scratch_shapes=[
+            pltpu.VMEM((rows, reach, lanes), F32),
+            pltpu.VMEM((2 * LANES, 2 * atoms), BF16),
+            pltpu.VMEM((2 * LANES, 2 * atoms), BF16),
+            pltpu.VMEM((2, block, atoms), F32),
+            pltpu.VMEM((3, 32, atoms), F32),
+        ],
+        compiler_params=pltpu.CompilerParams(vmem_limit_bytes=VMEM_LIMIT),
+        name="solve_interpolate",
+    )(here, moved.reshape(rows, parts * z_local, lanes), fh, fl, bh, bl, az, sz, col, sq, step, qm_table)
+
+
+def reduce_kernel(count_z, count_y, part_ref, out_ref, land_ref, send_sem, recv_sem):
+    p = lax.axis_index("gz")
+    y = lax.axis_index("gy")
+    me = p * count_y + y
+    total = count_z * count_y
+    width = out_ref.shape[1]
+    barrier = pltpu.get_barrier_semaphore()
+    for d in range(1, total):
+        other = lax.rem(me + d, total)
+        pl.semaphore_signal(barrier, inc=1, device_id=(other // count_y, lax.rem(other, count_y)), device_id_type=MESH)
+    pl.semaphore_wait(barrier, total - 1)
+    for d in range(1, total):
+        other = lax.rem(me + d, total)
+        pltpu.make_async_remote_copy(
+            src_ref=part_ref.at[other], dst_ref=land_ref.at[me], send_sem=send_sem, recv_sem=recv_sem,
+            device_id=(other // count_y, lax.rem(other, count_y)), device_id_type=MESH).start()
+    land_ref[me] = part_ref[me]
+    pltpu.make_async_remote_copy(
+        src_ref=land_ref.at[pl.ds(0, total - 1)], dst_ref=land_ref.at[pl.ds(0, total - 1)], send_sem=send_sem, recv_sem=recv_sem,
+        device_id=(p, 1 - y), device_id_type=MESH).wait()
+    out_ref[...] = jnp.sum(land_ref[...], axis=0)
+
+
+def reduce_forces(partial, count_z, count_y):
+    total, rows, width = partial.shape
+    vmem = pl.BlockSpec(memory_space=pltpu.VMEM)
+    return pl.pallas_call(
+        functools.partial(reduce_kernel, count_z, count_y),
+        in_specs=[vmem],
+        out_specs=vmem,
+        out_shape=jax.ShapeDtypeStruct((rows, width), F32),
+        scratch_shapes=[pltpu.VMEM((total, rows, width), F32), pltpu.SemaphoreType.DMA, pltpu.SemaphoreType.DMA],
+        compiler_params=pltpu.CompilerParams(collective_id=2, has_side_effects=True, vmem_limit_bytes=VMEM_LIMIT),
+        name="reduce_forces",
+    )(partial)
+
+
+def fast_shards(spread_weights, spread_base, qm_base, qm_frac, qm_charge):
+    points = GRID
+    count_z = lax.axis_size("gz")
+    count_y = lax.axis_size("gy")
+    z_local, y_local = points // count_z, points // count_y
+    kx_local = points // 2 // count_y
+    block = points // count_z
+    p = lax.axis_index("gz")
+    q = lax.axis_index("gy")
+    count = spread_weights.shape[1]
+    qm_count = qm_base.shape[1]
+
+    z_cell = spread_base[0] - p * z_local
+    y_cell = spread_base[1] - q * y_local
+    cells = jnp.stack([z_cell, y_cell, spread_base[2]]).astype(F32)
+    table = jnp.concatenate(
+        [spread_weights.reshape(ORDER * ORDER, ORDER, count).transpose(1, 0, 2).reshape(ORDER**3, count),
+         cells, jnp.zeros((5, count), F32)], axis=0)
+    own = order_by(y_cell, table)
+    lower = cells - jnp.asarray([z_local, 0, 0], F32)[:, None]
+    halo = order_by(y_cell + jnp.where(z_cell + ORDER > z_local, 0, y_local), table)
+    halo = jnp.concatenate([halo[: ORDER**3], halo[ORDER**3 : ORDER**3 + 1] - z_local, halo[ORDER**3 + 1 :]], axis=0)
+    qm = jnp.concatenate([qm_base.astype(F32), qm_frac, jnp.zeros((2, qm_count), F32)], axis=0)
+    tab, qm_all = gather(own, halo, qm, count_z, count_y)
+
+    lines = spread(tab, q * kx_local, kx_local, z_local, y_local, points)
+    send = transform_rows(lines, jnp.stack([p // PLANE, p % PLANE]), y_local, points)
+    moved = exchange(send)
+
+    qm_all = qm_all.transpose(1, 0, 2).reshape(8, count_z, count_y * qm_count)
+    w_z, d_z = spline_weights(qm_all[3])
+    w_y, d_y = spline_weights(qm_all[4])
+    w_x, d_x = spline_weights(qm_all[5])
+    qm_table = jnp.concatenate([qm_all[:3], w_z, d_z, w_y, d_y, w_x, d_x, jnp.zeros((5,) + qm_all.shape[1:], F32)], axis=0)
+    qm_table = qm_table.transpose(1, 0, 2)
+    kx_index = q * kx_local + jnp.arange(kx_local, dtype=jnp.int32)
+    ky_first = (p // 2) * block
+    ky_index = ky_first + jnp.arange(block, dtype=jnp.int32)
+    y_shift = jnp.where(p % 2 == 0, points, points - points // 4)
+    here = jnp.stack([q * kx_local, ky_first, y_shift])
+    partial = solve(moved, here, qm_table, kx_index, ky_index, points)
+    partial = partial.reshape(count_z, 8, count_y, qm_count).transpose(0, 2, 1, 3).reshape(count_z * count_y, 8, qm_count)
+    forces = reduce_forces(partial, count_z, count_y)
+    return -qm_charge * forces[:3]
+
+
+def quick(mesh):
+    return mesh.shape["gz"] == RING * PLANE and mesh.shape["gy"] == 2
+
+
 def solution(mesh):
     in_specs = (
         P(None, ("gz", "gy")),
@@ -305,4 +910,5 @@
         P(("gz", "gy")),
     )
     out_specs = P(None, ("gz", "gy"))
-    return jax.shard_map(shards, mesh=mesh, in_specs=in_specs, out_specs=out_specs, check_vma=False)
+    body = fast_shards if quick(mesh) else shards
+    return jax.shard_map(body, mesh=mesh, in_specs=in_specs, out_specs=out_specs, check_vma=False)

time: 884 us -> 350 us (0.40)
  blocking collectives: 287 us -> 0 us
  Pallas kernels: 55.5 us -> 324 us
  other arithmetic: 179 us -> 10.5 us
  waiting for transfers between devices: 134 us -> 0 us
  local copies, waits for them, and re-layouts: 113 us -> 10.2 us
  matrix products: 82.2 us -> 4.19 us
  between operations: 14.2 us -> 0.21 us
    all_gather x3 -> x0, blocking collectives: 287 us -> none  [the longest x1 184 us: shards(): all_base = lax.all_gather(qm_base, ('gz', 'gy'), axis=1, tiled=True)]
    pallas_call x1 -> x6, Pallas kernels: 55.5 us -> 324 us  [the longest x1 173 us: exchange(): pl.pallas_call(exchange_kernel, in_specs=[vmem], out_specs=vmem, out_shap...]
    unnamed x2 -> x0, waiting for transfers between devices: 134 us -> none
    dot_general x20 -> x2, matrix products: 82.2 us -> 4.19 us  [order_by(): return jnp.dot(table, moves, precision=HIGHEST)]
    all_to_all x1 -> x0, other arithmetic: 71.6 us -> none  [shards(): lax.all_to_all(packed, 'gz', split_axis=0, concat_axis=0, tiled=True)]
    dynamic_slice x32 -> x0, local copies, waits for them, and re-layouts: 28 us -> none  [shards(): partial = lax.map(one_slab, (lines, slab_base, slab_frac, starts))]
    sub x35 -> x1, other arithmetic: 26.1 us -> 0.01 us  [fast_shards(): halo[ORDER ** 3:ORDER ** 3 + 1] - z_local]
    unnamed x13 -> x12, local copies, waits for them, and re-layouts: 22.9 us -> 0.02 us
  transfers between devices with their start and end apart: 2 -> 0, of which waited for: 1 -> 0; matrix products, arithmetic and copies ran while one was open for 1% -> 0% of each run, Pallas kernels for 0% -> 0%
where the time goes in v1:
time: 350 us; the launch traced here: 349 us
  Pallas kernels  324 us (93%)
  other arithmetic  10.5 us (3%)
  local copies, waits for them, and re-layouts  10.2 us (3%)
  matrix products  4.19 us (1%)
    pallas_call x1, Pallas kernels, exchange(): pl.pallas_call(exchange_kernel, in_specs=[vmem], out_specs=vmem, out_shap...  173 us
    pallas_call x1, Pallas kernels, solve(): pl.pallas_call(functools.partial(solve_kernel, points, kx_local, block),...  52.1 us
    pallas_call x1, Pallas kernels, spread(): pl.pallas_call(functools.partial(lines_kernel, points, kx_local), grid_sp...  38.6 us
    pallas_call x1, Pallas kernels, gather(): pl.pallas_call(functools.partial(gather_kernel, count_z, count_y), out_sh...  24.8 us
    pallas_call x1, Pallas kernels, transform_rows(): pl.pallas_call(functools.partial(rows_kernel, z_local, groups), in_specs=...  24.4 us
    pallas_call x1, Pallas kernels, reduce_forces(): pl.pallas_call(functools.partial(reduce_kernel, count_z, count_y), in_spe...  10.6 us

profile of v1, /device:TPU:0, one launch (start us, length us, event | category | flops | bytes accessed | tf_op | source)
XLA Modules:
  0.0 348.7 jit_solution(14518479715387856211)
XLA Ops:
  0.0 0.7 pad_add_fusion.1.here_ref
  1.3 0.8 compare_select_fusion
  2.1 0.7 fusion.42
  2.8 0.8 convert_reduce_fusion.1
  3.6 1.0 reshape.628
  4.9 2.5 fusion.4.own_ref
  7.4 0.8 convert_reduce_fusion
  8.1 1.7 fusion.5
  9.9 0.7 pad_maximum_fusion.halo_ref
  10.7 0.7 maximum_maximum_fusion.3.qm_ref
  11.4 24.8 %gather_atoms.1 = (f32[2,2,72,1024]{3,2,1,0:T(8,128)}, f32[32,8,128]{2,1,0:T(8,128)}) custom-call(f32[72,1024]{1,0:T(8,128)} %fusion.4.own_ref, f32[72,1024]{1,0:T(8,128)} %pad_maximum_fusion.halo_ref, f32[8,128]{1,0:T(8,128)} %maximum_maximum_fusion.3.qm_ref), custom_call_target="tpu_custom_call" | custom-call | tf_op jit(solution)/shard_map/gather_atoms/pallas_call | solution.py:397
  36.2 0.9 round-nearest-even_convert_fusion
  38.4 38.6 %spread_lines.1 = f32[2,2,232,24,128]{4,3,2,1,0:T(8,128)} custom-call(s32[1]{0:T(128)} %bitcast.kx_ref, s32[64]{0:T(128)} %copy-done.1, s32[64]{0:T(128)} %fusion.39.count_ref, f32[2,2,72,1024]{3,2,1,0:T(8,128)} %get-tuple-element.7.tab_ref), custom_call_target="tpu_custom_call" | custom-call | tf_op jit(solution)/shard_map/spread_lines/pallas_call | solution.py:508
  77.0 24.4 %transform_rows.1 = f32[13824,128]{1,0:T(8,128)} custom-call(s32[2]{0:T(128)} %pad_add_fusion.2.here_ref, f32[2,11136,128]{2,1,0:T(8,128)} %bitcast.28, bf16[384,464]{1,0:T(8,128)(2,1)} %constant.198.clone.high_ref, bf16[384,464]{1,0:T(8,128)(2,1)} %constant.199.clone.low_ref), custom_call_target="tpu_custom_call" | custom-call | tf_op jit(solution)/shard_map/transform_rows/pallas_call | solution.py:572
  101.4 173.1 %exchange_blocks.1 = f32[36,16,24,128]{3,2,1,0:T(8,128)} custom-call(f32[4,4,36,24,128]{4,3,2,1,0:T(8,128)} %bitcast.30), custom_call_target="tpu_custom_call" | custom-call | tf_op jit(solution)/shard_map/exchange_blocks/pallas_call | solution.py:661
  274.5 0.7 broadcast_in_dim.52.az_ref
  275.3 0.7 broadcast_in_dim.53.sz_ref
  278.1 1.3 broadcast_in_dim.56.step_ref
  279.9 3.3 concatenate.42
  283.2 52.1 %solve_interpolate.1 = f32[16,8,256]{2,1,0:T(8,128)} custom-call(s32[3]{0:T(128)} %pad_add_fusion.1.here_ref, f32[36,384,128]{2,1,0:T(8,128)} %bitcast.29, bf16[384,384]{1,0:T(8,128)(2,1)} %constant.200.clone.fh_ref, bf16[384,384]{1,0:T(8,128)(2,1)} %constant.201.clone.fl_ref, bf16[392,384]{1,0:T(8,128)(2,1)} %constant.202.clone.bh_ref, ...), custom_call_target="tpu_custom_call" | custom-call | tf_op jit(solution)/shard_map/solve_interpolate/pallas_call | solution.py:800
  335.3 0.9 fusion.43
  336.1 0.7 pad_maximum_fusion.1
  336.8 10.6 %reduce_forces.1 = f32[8,128]{1,0:T(8,128)} custom-call(f32[32,8,128]{2,1,0:T(8,128)} %bitcast.33), custom_call_target="tpu_custom_call" | custom-call | tf_op jit(solution)/shard_map/reduce_forces/pallas_call | solution.py:843
  347.4 1.3 slice_multiply_fusion
  (63 shorter events, 4.8 us)
Async XLA Ops:
  0.0 37.5 %copy-start.4 = (s32[2]{0:T(128)S(1)}, s32[2]{0:T(128)}, u32[]{:S(2)}) copy-start(s32[2]{0:T(128)} %constant.197.clone) | copy-start | bytes 28
  0.0 10.7 %copy-start.2 = (f32[3,128]{1,0:T(4,128)S(1)}, f32[3,128]{1,0:T(4,128)}, u32[]{:S(2)}) copy-start(f32[3,128]{1,0:T(4,128)} %param.16) | copy-start | bytes 4612
  0.0 10.7 %copy-start.3 = (s32[3,128]{1,0:T(4,128)S(1)}, s32[3,128]{1,0:T(4,128)}, u32[]{:S(2)}) copy-start(s32[3,128]{1,0:T(4,128)} %param.15) | copy-start | bytes 4612
  37.5 0.9 copy-start.1
  101.4 178.0 %copy-start = (f32[32,8,128]{2,1,0:T(8,128)S(1)}, f32[32,8,128]{2,1,0:T(8,128)}, u32[]{:S(2)}) copy-start(f32[32,8,128]{2,1,0:T(8,128)} %get-tuple-element.8) | copy-start | bytes 393220
  283.2 64.2 %copy-start.5 = (f32[128]{0:T(128)S(1)}, f32[128]{0:T(128)}, u32[]{:S(2)}) copy-start(f32[128]{0:T(128)} %param.17) | copy-start | bytes 1540

commit v2 on v0

--- a/solution.py
+++ b/solution.py
@@ -1,7 +1,9 @@
+import functools
 import math
 
 import jax
 import jax.numpy as jnp
+import numpy as np
 from jax import lax
 from jax.experimental import pallas as pl
 from jax.experimental.pallas import tpu as pltpu
@@ -296,6 +298,557 @@
     return -qm_charge * forces
 
 
+MESH = pl.DeviceIdType.MESH
+RING = 4
+PLANE = 4
+LANES = 128
+F32 = jnp.float32
+BF16 = jnp.bfloat16
+VMEM_LIMIT = 62 * 2**20
+
+
+def split_table(table):
+    high = table.astype(np.float32).astype(BF16)
+    low = (table - high.astype(np.float64)).astype(np.float32).astype(BF16)
+    return jnp.asarray(high), jnp.asarray(low)
+
+
+def split(value):
+    high = value.astype(BF16)
+    return high, (value - high.astype(F32)).astype(BF16)
+
+
+def dot3(a_high, a_low, b_high, b_low):
+    total = jnp.dot(a_high, b_high, preferred_element_type=F32)
+    total += jnp.dot(a_low, b_high, preferred_element_type=F32)
+    return total + jnp.dot(a_high, b_low, preferred_element_type=F32)
+
+
+def trig(units, points):
+    rest = units - points * jnp.floor((units + 0.5) * (1.0 / points))
+    quarter = points // 4
+    turn = jnp.floor((rest + quarter / 2) * (1.0 / quarter))
+    angle = (rest - quarter * turn) * (2.0 * math.pi / points)
+    square = angle * angle
+    sine = angle * (1.0 + square * (-1.0 / 6 + square * (1.0 / 120 + square * (-1.0 / 5040 + square / 362880))))
+    cosine = 1.0 + square * (-0.5 + square * (1.0 / 24 + square * (-1.0 / 720 + square * (1.0 / 40320))))
+    odd = (turn == 1.0) | (turn == 3.0)
+    first = jnp.where(odd, sine, cosine)
+    second = jnp.where(odd, cosine, sine)
+    first = jnp.where((turn == 1.0) | (turn == 2.0), -first, first)
+    second = jnp.where((turn == 2.0) | (turn == 3.0), -second, second)
+    return first, second
+
+
+def order_by(key, table):
+    count = key.shape[0]
+    order = jnp.arange(count, dtype=jnp.int32)
+    before = (key[:, None] < key[None, :]) | ((key[:, None] == key[None, :]) & (order[:, None] < order[None, :]))
+    rank = jnp.sum(before.astype(jnp.int32), axis=0)
+    moves = (rank[:, None] == order[None, :]).astype(F32)
+    return jnp.dot(table, moves, precision=HIGHEST)
+
+
+def gather_kernel(own_ref, qm_ref, tab_ref, all_ref, zs, zr, xs, xr, ys, yr, fs, fr, gs, gr, qm_send, qm_recv):
+    p = lax.axis_index("gz")
+    y = lax.axis_index("gy")
+    me = p * 2 + y
+    total = RING * PLANE * 2
+    ring, spot = p // PLANE, lax.rem(p, PLANE)
+    x, core = spot // 2, lax.rem(spot, 2)
+    barrier = pltpu.get_barrier_semaphore()
+    for d in range(1, total):
+        other = lax.rem(me + d, total)
+        pl.semaphore_signal(barrier, inc=1, device_id=(other // 2, lax.rem(other, 2)), device_id_type=MESH)
+    pl.semaphore_wait(barrier, total - 1)
+
+    def place(z, xx, yy):
+        return (z * 2 + xx) * 2 + yy
+
+    def copy(src, dst, s, r, device):
+        return pltpu.make_async_remote_copy(src_ref=src, dst_ref=dst, send_sem=s, recv_sem=r, device_id=device, device_id_type=MESH)
+
+    above = (p + PLANE, y)
+    below = (p - PLANE, y)
+    aside = (ring * PLANE + (1 - x) * 2 + core, y)
+    over = (p, 1 - y)
+    cut = tab_ref.shape[1] // 16 * 8
+    tab_ref[place(ring, x, y)] = own_ref[...]
+    for d in range(1, total):
+        other = lax.rem(me + d, total)
+        copy(qm_ref, all_ref.at[me], qm_send, qm_recv, (other // 2, lax.rem(other, 2))).start()
+    all_ref[me] = qm_ref[...]
+    lower = (RING - 1 - ring) // 2
+    near = ring + 1 - 2 * lax.rem(ring, 2)
+    order = [ring, near, 1 + lower, (RING - 1) * lower]
+
+    def along(z, i):
+        src = own_ref if i == 0 else tab_ref.at[place(z, x, y)]
+        dst = tab_ref.at[place(z, x, y)]
+        return copy(src, dst, zs.at[0, z], zr.at[z], above), copy(src, dst, zs.at[1, z], zr.at[z], below)
+
+    def flat(z, i):
+        src = own_ref if i == 0 else tab_ref.at[place(z, x, y)]
+        dst = tab_ref.at[place(z, x, y)]
+        return copy(src, dst, xs.at[z], xr.at[z], aside), copy(src, dst, ys.at[z], yr.at[z], over)
+
+    def turn(z):
+        first = tab_ref.at[place(z, 1 - x, y), pl.ds(0, cut)]
+        second = tab_ref.at[place(z, x, 1 - y), pl.ds(cut, tab_ref.shape[1] - cut)]
+        return copy(first, first, fs.at[z], fr.at[z], over), copy(second, second, gs.at[z], gr.at[z], aside)
+
+    def corner(z):
+        first = tab_ref.at[place(z, 1 - x, 1 - y), pl.ds(0, cut)]
+        second = tab_ref.at[place(z, 1 - x, 1 - y), pl.ds(cut, tab_ref.shape[1] - cut)]
+        return copy(first, first, fs.at[z], fr.at[z], over), copy(second, second, gs.at[z], gr.at[z], aside)
+
+    def upward(z):
+        return (z <= ring) & (ring < RING - 1)
+
+    def downward(z):
+        return (z >= ring) & (ring > 0)
+
+    def relay(z):
+        mine = tab_ref.at[place(z, 1 - x, y)]
+        theirs = tab_ref.at[place(z, x, 1 - y)]
+        copy(mine, mine, xs.at[z], xr.at[z], aside).wait_recv()
+        copy(theirs, theirs, ys.at[z], yr.at[z], over).wait_recv()
+        for c in turn(z):
+            c.start()
+
+    for i, z in enumerate(order):
+        up, down = along(z, i)
+        if i:
+            up.wait_recv()
+
+        @pl.when(upward(z))
+        def _():
+            up.start()
+
+        @pl.when(downward(z))
+        def _():
+            down.start()
+
+        for c in flat(z, i):
+            c.start()
+        if i:
+            relay(order[i - 1])
+    relay(order[-1])
+    for i, z in enumerate(order):
+        for c in corner(z):
+            c.wait_recv()
+    for i, z in enumerate(order):
+        up, down = along(z, i)
+
+        @pl.when(upward(z))
+        def _():
+            up.wait_send()
+
+        @pl.when(downward(z))
+        def _():
+            down.wait_send()
+
+        for c in flat(z, i) + turn(z):
+            c.wait_send()
+    rest = all_ref.at[pl.ds(0, total - 1)]
+    copy(rest, rest, qm_send, qm_recv, over).wait()
+
+
+def gather(own, qm):
+    vmem = pl.BlockSpec(memory_space=pltpu.VMEM)
+    ring = pltpu.SemaphoreType.DMA((RING,))
+    single = pltpu.SemaphoreType.DMA
+    return pl.pallas_call(
+        gather_kernel,
+        out_shape=(
+            jax.ShapeDtypeStruct((RING * 4,) + own.shape, F32),
+            jax.ShapeDtypeStruct((RING * PLANE * 2,) + qm.shape, F32),
+        ),
+        in_specs=[vmem] * 2,
+        out_specs=(vmem, vmem),
+        scratch_shapes=[pltpu.SemaphoreType.DMA((2, RING))] + [ring] * 9 + [single, single],
+        compiler_params=pltpu.CompilerParams(collective_id=0, has_side_effects=True, vmem_limit_bytes=VMEM_LIMIT),
+        name="gather_atoms",
+    )(own, qm)
+
+
+Z_STEP = 6
+BLOCK = 256
+
+
+def lines_kernel(points, kx_local, z_used, kx_ref, first_ref, count_ref, tab_ref, th_ref, tl_ref, out_ref, grid_ref):
+    slab, half, block = pl.program_id(0), pl.program_id(1), pl.program_id(2)
+    blocks = pl.num_programs(2)
+    modes = 2 * kx_local
+    part = LANES // 2
+    rows = ORDER * ORDER
+
+    @pl.when((half == 0) & (block == 0))
+    def _():
+        grid_ref[...] = jnp.zeros_like(grid_ref)
+
+    lane = lax.broadcasted_iota(jnp.int32, (1, LANES), 1)
+    mode = lax.broadcasted_iota(jnp.int32, (modes, LANES), 0)
+    sine = mode >= kx_local
+    kx = (kx_ref[0] + jnp.where(sine, mode - kx_local, mode)).astype(F32)
+    shift = jnp.where(sine, points - points // 4, points).astype(F32)
+    steps = [trig(kx * float(c), points) for c in range(ORDER)]
+    wide = lax.broadcasted_iota(jnp.int32, (1, 2 * LANES), 1)
+    y_shift = wide // part
+    y_rows = lax.broadcasted_iota(jnp.int32, (2 * LANES, 2 * LANES), 0)
+    z_rows = lax.broadcasted_iota(jnp.int32, (8, 2 * LANES), 0)
+    base = ((slab * 2 + half) * blocks + block) * (BLOCK // part)
+    most = count_ref[base]
+    for g in range(1, BLOCK // part):
+        most = jnp.maximum(most, count_ref[base + g])
+
+    def step(it, carry):
+        for g in range(BLOCK // part):
+            tab = tab_ref[:, (g // 2) * LANES : (g // 2 + 1) * LANES]
+
+            def pair(even, odd):
+                if g % 2 == 0:
+                    return jnp.where(lane < part, even, pltpu.roll(odd, part, 1))
+                return jnp.where(lane < part, pltpu.roll(even, part, 1), odd)
+
+            weights = jnp.concatenate(
+                [pair(tab[0:rows], tab[rows : 2 * rows]), pair(tab[2 * rows : 3 * rows], tab[3 * rows : 4 * rows])], axis=1)
+            spots = tab[4 * rows : 4 * rows + 8]
+            spots = pair(spots, spots)
+            twice = jnp.concatenate([spots, spots], axis=1).astype(jnp.int32)
+            z_first = first_ref[base + g] + it * Z_STEP
+            live = it < count_ref[base + g]
+            off = z_rows + jnp.where(live, z_first, 4 * points) - twice[0:1]
+            z_first = jnp.minimum(z_first, z_used - 1)
+            cosine, sinus = trig(kx * spots[2:3] + shift, points)
+            waves, picks = [], []
+            for c in range(ORDER):
+                wave = cosine * steps[c][0] - sinus * steps[c][1] if c else cosine
+                waves.append(jnp.concatenate([wave, wave], axis=1))
+                pick = jnp.zeros((8, 2 * LANES), F32)
+                for a in range(ORDER):
+                    pick = jnp.where(off == a, weights[a * ORDER + c : a * ORDER + c + 1], pick)
+                picks.append(pick)
+            pieces = []
+            for z in range(Z_STEP):
+                value = picks[0][z : z + 1] * waves[0]
+                for c in range(1, ORDER):
+                    value += picks[c][z : z + 1] * waves[c]
+                pieces.append(value)
+            high, low = split(jnp.concatenate(pieces, axis=0))
+            hits = jnp.where(y_rows == twice[1:2] + y_shift, 1.0, 0.0).astype(BF16)
+            across = (((1,), (1,)), ((), ()))
+            total = lax.dot_general(high, hits, across, preferred_element_type=F32)
+            total += lax.dot_general(low, hits, across, preferred_element_type=F32)
+            grid_ref[half, pl.ds(pl.multiple_of(z_first * modes, 8), Z_STEP * modes), :] += total
+        return carry
+
+    lax.fori_loop(0, most, step, 0)
+
+    @pl.when((half == 1) & (block == blocks - 1))
+    def _():
+        cuts = 3
+        size = z_used * modes // cuts
+
+        def chunk(i, carry):
+            at = pl.multiple_of(i * size, 8)
+            total = None
+            for h in range(2):
+                high, low = split(grid_ref[h, pl.ds(at, size), :])
+                found = dot3(high, low, th_ref[h], tl_ref[h])
+                total = found if total is None else total + found
+            for t in range(4):
+                out_ref[t // 2, t % 2, pl.ds(at, size), :] = total[:, t * LANES : (t + 1) * LANES]
+            return carry
+
+        lax.fori_loop(0, cuts, chunk, 0)
+
+
+def spread(tab, kx_first, kx_local, z_local, y_local, points):
+    tables, rows, count = tab.shape
+    slabs = tables // 2
+    part = LANES // 2
+    z_used = z_local + ORDER - 1
+    modes = 2 * kx_local
+    z_cell = jnp.round(tab[:, 4 * ORDER * ORDER]).astype(jnp.int32).reshape(tables, count // part, part)
+    first = jnp.min(z_cell, axis=-1)
+    counts = (jnp.max(z_cell, axis=-1) - first + ORDER + Z_STEP - 1) // Z_STEP
+    k = np.arange(points // 2)
+    cell = (np.arange(2)[:, None] * y_local + np.arange(2 * LANES)[None, :]) % points
+    angle = 2.0 * np.pi / points * ((cell[:, :, None] * k) % points)
+    table = np.zeros((2, 2 * LANES, 2, 2 * LANES))
+    table[:, :, 0, : points // 2] = np.cos(angle)
+    table[:, :, 1, : points // 2] = np.sin(angle)
+    th, tl = split_table(table.reshape(2, 2 * LANES, 4 * LANES))
+    whole = lambda s, h, b, *_: (0, 0, 0)
+    return pl.pallas_call(
+        functools.partial(lines_kernel, points, kx_local, z_used),
+        grid_spec=pltpu.PrefetchScalarGridSpec(
+            num_scalar_prefetch=3,
+            grid=(slabs, 2, count // BLOCK),
+            in_specs=[
+                pl.BlockSpec((None, rows, BLOCK), lambda s, h, b, *_: (s * 2 + h, 0, b)),
+                pl.BlockSpec(th.shape, whole),
+                pl.BlockSpec(tl.shape, whole),
+            ],
+            out_specs=pl.BlockSpec((2, 2, None, z_used * modes, LANES), lambda s, h, b, *_: (0, 0, s, 0, 0)),
+            scratch_shapes=[pltpu.VMEM((2, (z_used + Z_STEP - 1) * modes, 2 * LANES), F32)],
+        ),
+        out_shape=jax.ShapeDtypeStruct((2, 2, slabs, z_used * modes, LANES), F32),
+        compiler_params=pltpu.CompilerParams(dimension_semantics=("arbitrary",) * 3, vmem_limit_bytes=VMEM_LIMIT),
+        name="spread_lines",
+    )(kx_first.reshape(1), first.reshape(-1), counts.reshape(-1), tab, th, tl)
+
+
+def swap_kernel(lines_ref, out_ref, send_sem, recv_sem):
+    p = lax.axis_index("gz")
+    y = lax.axis_index("gy")
+    core = lax.rem(p, 2)
+    other = p + 1 - 2 * core
+    barrier = pltpu.get_barrier_semaphore()
+    pl.semaphore_signal(barrier, inc=1, device_id=(other, y), device_id_type=MESH)
+    pl.semaphore_wait(barrier, 1)
+    copy = pltpu.make_async_remote_copy(
+        src_ref=lines_ref.at[1 - core], dst_ref=out_ref.at[:, core], send_sem=send_sem, recv_sem=recv_sem,
+        device_id=(other, y), device_id_type=MESH)
+    copy.start()
+
+    def keep(i, carry):
+        for t in range(2):
+            out_ref[t, core, i] = lines_ref[core, t, i]
+        return carry
+
+    lax.fori_loop(0, lines_ref.shape[2], keep, 0)
+    copy.wait()
+
+
+def swap(lines):
+    types, tiles, slabs, deep, lanes = lines.shape
+    vmem = pl.BlockSpec(memory_space=pltpu.VMEM)
+    out = pl.pallas_call(
+        swap_kernel,
+        in_specs=[vmem],
+        out_specs=vmem,
+        out_shape=jax.ShapeDtypeStruct((tiles, 2, slabs, deep, lanes), F32),
+        scratch_shapes=[pltpu.SemaphoreType.DMA, pltpu.SemaphoreType.DMA],
+        compiler_params=pltpu.CompilerParams(collective_id=1, has_side_effects=True, vmem_limit_bytes=VMEM_LIMIT),
+        name="swap_modes",
+    )(lines)
+    return out.reshape(tiles, 2 * slabs * deep, lanes)
+
+
+def solve_kernel(points, kx_local, here_ref, x_ref, fh_ref, fl_ref, bh_ref, bl_ref, az_ref, sz_ref, col_ref, sq_ref, step_ref, qm_ref, out_ref, pot_ref, wave_h, wave_l, wx_ref, acc_ref):
+    modes = 2 * kx_local
+    deep = x_ref.shape[1] // modes
+    half = points // 2
+    slabs = qm_ref.shape[0]
+    z_local = points // slabs
+    atoms = qm_ref.shape[2]
+    kx_first, y_shift = here_ref[0], here_ref[1]
+
+    def convolve(m, carry):
+        data = jnp.concatenate([x_ref[t, pl.ds(m, deep, stride=modes), :] for t in range(2)], axis=1)
+        high, low = split(data)
+        coef = dot3(fh_ref[...], fl_ref[...], high, low)
+        total = sz_ref[...] + sq_ref[pl.ds(m, 1), :]
+        keep = total > 0.0
+        value = az_ref[...] * col_ref[pl.ds(m, 1), :] / jnp.where(keep, total, 1.0)
+        green = jnp.where(keep, value, 0.0)
+        high, low = split(coef * jnp.concatenate([green, green], axis=0))
+        pot_ref[m] = dot3(bh_ref[...], bl_ref[...], high, low)
+        return carry
+
+    lax.fori_loop(0, modes, convolve, 0)
+    span = 4 * 8
+    wave_h[half:] = jnp.zeros((2 * LANES - half, 2 * atoms), BF16)
+    wave_l[half:] = jnp.zeros((2 * LANES - half, 2 * atoms), BF16)
+    ky = lax.broadcasted_iota(jnp.int32, (half, atoms), 0).astype(F32)
+    mode = lax.broadcasted_iota(jnp.int32, (modes, atoms), 0)
+    sine = mode >= kx_local
+    kx = (kx_first + jnp.where(sine, mode - kx_local, mode)).astype(F32)
+    x_shift = jnp.where(sine, points - points // 4, points).astype(F32)
+
+    def slab(p, carry):
+        qm = qm_ref[p]
+        row = lambda i: qm[i : i + 1]
+        cosine, sinus = trig(ky * row(1) + y_shift.astype(F32), points)
+        for k, at in ((0, 11), (1, 15)):
+            real = imag = None
+            for c in range(ORDER):
+                sc = jnp.concatenate([step_ref[c]] * (atoms // LANES), axis=1)
+                ss = jnp.concatenate([step_ref[ORDER + c]] * (atoms // LANES), axis=1)
+                real = row(at + c) * sc if real is None else real + row(at + c) * sc
+                imag = row(at + c) * ss if imag is None else imag + row(at + c) * ss
+            high, low = split(cosine * real - sinus * imag)
+            wave_h[0:half, k * atoms : (k + 1) * atoms] = high
+            wave_l[0:half, k * atoms : (k + 1) * atoms] = low
+        plain_x = slope_x = jnp.zeros((modes, atoms), F32)
+        for c in range(ORDER):
+            wave, _ = trig(kx * (row(2) + float(c)) + x_shift, points)
+            plain_x += row(19 + c) * wave
+            slope_x += row(23 + c) * wave
+        wx_ref[0] = plain_x
+        wx_ref[1] = slope_x
+        z_first = pl.multiple_of(p * z_local, 8)
+        acc_ref[...] = jnp.zeros_like(acc_ref)
+        for g in range(modes // 8):
+            tiles = [pot_ref[g * 8 + i, pl.ds(z_first, span), :] for i in range(8)]
+            high, low = split(jnp.concatenate(tiles, axis=0))
+            along = dot3(high, low, wave_h[...], wave_l[...])
+            for i in range(8):
+                r = g * 8 + i
+                value, slope = along[i * span : (i + 1) * span, :atoms], along[i * span : (i + 1) * span, atoms:]
+                wx, dx = wx_ref[0, r : r + 1], wx_ref[1, r : r + 1]
+                acc_ref[0] += value * wx
+                acc_ref[1] += slope * wx
+                acc_ref[2] += value * dx
+        off = lax.broadcasted_iota(jnp.int32, (span, atoms), 0) + z_first - row(0).astype(jnp.int32)
+        wz = dz = jnp.zeros((span, atoms), F32)
+        for a in range(ORDER):
+            wz = jnp.where(off == a, row(3 + a), wz)
+            dz = jnp.where(off == a, row(7 + a), dz)
+        total = lambda v: jnp.sum(v, axis=0, keepdims=True)
+        out_ref[p] = jnp.concatenate(
+            [total(acc_ref[0] * dz), total(acc_ref[1] * wz), total(acc_ref[2] * wz), jnp.zeros((5, atoms), F32)], axis=0)
+        return carry
+
+    lax.fori_loop(0, slabs, slab, 0)
+
+
+def solve(lines, here, qm_table, kx_index, points):
+    tiles, deep, lanes = lines.shape
+    kx_local = kx_index.shape[0]
+    modes = 2 * kx_local
+    half = points // 2
+    slabs, _, atoms = qm_table.shape
+    z_local = points // slabs
+    z_used = z_local + ORDER - 1
+    k = np.arange(half)
+
+    def waves(z):
+        angle = 2.0 * np.pi / points * ((k[:, None] * z[None, :]) % points)
+        return np.concatenate([np.cos(angle), np.sin(angle)], axis=0)
+
+    core, pair, plane = np.meshgrid(np.arange(2), np.arange(slabs // 2), np.arange(z_used), indexing="ij")
+    fh, fl = split_table(waves((((pair * 2 + core) * z_local + plane) % points).reshape(-1)))
+    reach = points + 8
+    bh, bl = split_table(waves(np.arange(reach) % points).T)
+
+    def parts_of(index):
+        square, spline, _ = moduli(index, points)
+        decay = jnp.exp(-(math.pi * math.pi / (SPLITTING * SPLITTING)) * square)
+        return square, spline * decay * jnp.where(index == 0, 1.0, 2.0)
+
+    z_sq, z_fac = parts_of(jnp.asarray(k, jnp.int32))
+    x_sq, x_fac = parts_of(jnp.concatenate([kx_index, kx_index]))
+    pad = (0, 2 * lanes - half)
+    y_sq, y_fac = jnp.pad(z_sq, pad), jnp.pad(z_fac, pad)
+    col = x_fac[:, None] * y_fac[None, :] * (1.0 / (math.pi * float(points) ** 3))
+    sq = x_sq[:, None] + y_sq[None, :]
+    az = jnp.broadcast_to(z_fac[:, None], (half, 2 * lanes))
+    sz = jnp.broadcast_to(z_sq[:, None], (half, 2 * lanes))
+    turn = 2.0 * np.pi / points * (np.arange(ORDER)[:, None] * k[None, :] % points)
+    step = np.concatenate([np.cos(turn), np.sin(turn)], axis=0)
+    step = jnp.broadcast_to(jnp.asarray(step[:, :, None], F32), step.shape + (lanes,))
+    vmem = pl.BlockSpec(memory_space=pltpu.VMEM)
+    return pl.pallas_call(
+        functools.partial(solve_kernel, points, kx_local),
+        in_specs=[pl.BlockSpec(memory_space=pltpu.SMEM)] + [vmem] * 11,
+        out_specs=vmem,
+        out_shape=jax.ShapeDtypeStruct((slabs, 8, atoms), F32),
+        scratch_shapes=[
+            pltpu.VMEM((modes, reach, 2 * lanes), F32),
+            pltpu.VMEM((2 * lanes, 2 * atoms), BF16),
+            pltpu.VMEM((2 * lanes, 2 * atoms), BF16),
+            pltpu.VMEM((2, modes, atoms), F32),
+            pltpu.VMEM((3, 32, atoms), F32),
+        ],
+        compiler_params=pltpu.CompilerParams(vmem_limit_bytes=VMEM_LIMIT),
+        name="solve_interpolate",
+    )(here, lines, fh, fl, bh, bl, az, sz, col, sq, step, qm_table)
+
+
+def reduce_kernel(count_z, count_y, part_ref, out_ref, land_ref, send_sem, recv_sem):
+    p = lax.axis_index("gz")
+    y = lax.axis_index("gy")
+    me = p * count_y + y
+    total = count_z * count_y
+    width = out_ref.shape[1]
+    barrier = pltpu.get_barrier_semaphore()
+    for d in range(1, total):
+        other = lax.rem(me + d, total)
+        pl.semaphore_signal(barrier, inc=1, device_id=(other // count_y, lax.rem(other, count_y)), device_id_type=MESH)
+    pl.semaphore_wait(barrier, total - 1)
+    for d in range(1, total):
+        other = lax.rem(me + d, total)
+        pltpu.make_async_remote_copy(
+            src_ref=part_ref.at[other], dst_ref=land_ref.at[me], send_sem=send_sem, recv_sem=recv_sem,
+            device_id=(other // count_y, lax.rem(other, count_y)), device_id_type=MESH).start()
+    land_ref[me] = part_ref[me]
+    pltpu.make_async_remote_copy(
+        src_ref=land_ref.at[pl.ds(0, total - 1)], dst_ref=land_ref.at[pl.ds(0, total - 1)], send_sem=send_sem, recv_sem=recv_sem,
+        device_id=(p, 1 - y), device_id_type=MESH).wait()
+    out_ref[...] = jnp.sum(land_ref[...], axis=0)
+
+
+def reduce_forces(partial, count_z, count_y):
+    total, rows, width = partial.shape
+    vmem = pl.BlockSpec(memory_space=pltpu.VMEM)
+    return pl.pallas_call(
+        functools.partial(reduce_kernel, count_z, count_y),
+        in_specs=[vmem],
+        out_specs=vmem,
+        out_shape=jax.ShapeDtypeStruct((rows, width), F32),
+        scratch_shapes=[pltpu.VMEM((total, rows, width), F32), pltpu.SemaphoreType.DMA, pltpu.SemaphoreType.DMA],
+        compiler_params=pltpu.CompilerParams(collective_id=2, has_side_effects=True, vmem_limit_bytes=VMEM_LIMIT),
+        name="reduce_forces",
+    )(partial)
+
+
+def fast_shards(spread_weights, spread_base, qm_base, qm_frac, qm_charge):
+    points = GRID
+    count_z = lax.axis_size("gz")
+    count_y = lax.axis_size("gy")
+    z_local, y_local = points // count_z, points // count_y
+    kx_local = points // (RING * PLANE * 2)
+    p = lax.axis_index("gz")
+    q = lax.axis_index("gy")
+    count = spread_weights.shape[1]
+    qm_count = qm_base.shape[1]
+
+    z_cell = spread_base[0] - p * z_local
+    y_cell = spread_base[1] - q * y_local
+    cells = jnp.stack([z_cell, y_cell, spread_base[2]]).astype(F32)
+    table = jnp.concatenate(
+        [spread_weights.reshape(ORDER, ORDER, ORDER, count).transpose(1, 0, 2, 3).reshape(ORDER**3, count),
+         cells, jnp.zeros((5, count), F32)], axis=0)
+    own = order_by(z_cell, table)
+    qm = jnp.concatenate([qm_base.astype(F32), qm_frac, jnp.zeros((2, qm_count), F32)], axis=0)
+    tab, qm_all = gather(own, qm)
+
+    kx_first = ((p // 2) * count_y + q) * kx_local
+    lines = spread(tab, kx_first, kx_local, z_local, y_local, points)
+    lines = swap(lines)
+
+    qm_all = qm_all.transpose(1, 0, 2).reshape(8, count_z, count_y * qm_count)
+    w_z, d_z = spline_weights(qm_all[3])
+    w_y, d_y = spline_weights(qm_all[4])
+    w_x, d_x = spline_weights(qm_all[5])
+    qm_table = jnp.concatenate([qm_all[:3], w_z, d_z, w_y, d_y, w_x, d_x, jnp.zeros((5,) + qm_all.shape[1:], F32)], axis=0)
+    qm_table = qm_table.transpose(1, 0, 2)
+    kx_index = kx_first + jnp.arange(kx_local, dtype=jnp.int32)
+    y_shift = jnp.where(p % 2 == 0, points, points - points // 4)
+    here = jnp.stack([kx_first, y_shift])
+    partial = solve(lines, here, qm_table, kx_index, points)
+    partial = partial.reshape(count_z, 8, count_y, qm_count).transpose(0, 2, 1, 3).reshape(count_z * count_y, 8, qm_count)
+    forces = reduce_forces(partial, count_z, count_y)
+    return -qm_charge * forces[:3]
+
+
+def quick(mesh):
+    return mesh.shape["gz"] == RING * PLANE and mesh.shape["gy"] == 2
+
+
 def solution(mesh):
     in_specs = (
         P(None, ("gz", "gy")),
@@ -305,4 +858,5 @@
         P(("gz", "gy")),
     )
     out_specs = P(None, ("gz", "gy"))
-    return jax.shard_map(shards, mesh=mesh, in_specs=in_specs, out_specs=out_specs, check_vma=False)
+    body = fast_shards if quick(mesh) else shards
+    return jax.shard_map(body, mesh=mesh, in_specs=in_specs, out_specs=out_specs, check_vma=False)

time: 884 us -> 242 us (0.27)
  blocking collectives: 287 us -> 0 us
  other arithmetic: 179 us -> 9.9 us
  Pallas kernels: 55.5 us -> 220 us
  waiting for transfers between devices: 134 us -> 0 us
  local copies, waits for them, and re-layouts: 113 us -> 8.45 us
  matrix products: 82.2 us -> 2.46 us
  between operations: 14.2 us -> 0.15 us
    all_gather x3 -> x0, blocking collectives: 287 us -> none  [the longest x1 184 us: shards(): all_base = lax.all_gather(qm_base, ('gz', 'gy'), axis=1, tiled=True)]
    pallas_call x1 -> x5, Pallas kernels: 55.5 us -> 220 us  [the longest x1 76 us: spread(): pl.pallas_call(functools.partial(lines_kernel, points, kx_local, z_used),...]
    unnamed x2 -> x0, waiting for transfers between devices: 134 us -> none
    dot_general x20 -> x1, matrix products: 82.2 us -> 2.46 us  [order_by(): return jnp.dot(table, moves, precision=HIGHEST)]
    all_to_all x1 -> x0, other arithmetic: 71.6 us -> none  [shards(): lax.all_to_all(packed, 'gz', split_axis=0, concat_axis=0, tiled=True)]
    dynamic_slice x32 -> x0, local copies, waits for them, and re-layouts: 28 us -> none  [shards(): partial = lax.map(one_slab, (lines, slab_base, slab_frac, starts))]
    sub x35 -> x1, other arithmetic: 26.1 us -> 0.84 us  [fast_shards(): y_cell = spread_base[1] - q * y_local]
    unnamed x13 -> x8, local copies, waits for them, and re-layouts: 22.9 us -> 0.01 us
  transfers between devices with their start and end apart: 2 -> 0, of which waited for: 1 -> 0; matrix products, arithmetic and copies ran while one was open for 1% -> 0% of each run, Pallas kernels for 0% -> 0%
where the time goes in v2:
time: 242 us; the launch traced here: 241 us
  Pallas kernels  220 us (91%)
  other arithmetic  9.9 us (4%)
  local copies, waits for them, and re-layouts  8.45 us (3%)
  matrix products  2.46 us (1%)
    pallas_call x1, Pallas kernels, spread(): pl.pallas_call(functools.partial(lines_kernel, points, kx_local, z_used),...  76 us
    pallas_call x1, Pallas kernels, solve(): pl.pallas_call(functools.partial(solve_kernel, points, kx_local), in_spec...  62.7 us
    pallas_call x1, Pallas kernels, gather(): pl.pallas_call(gather_kernel, out_shape=(jax.ShapeDtypeStruct((RING * 4,)...  54.7 us
    pallas_call x1, Pallas kernels, swap(): pl.pallas_call(swap_kernel, in_specs=[vmem], out_specs=vmem, out_shape=ja...  16.8 us
    pallas_call x1, Pallas kernels, reduce_forces(): pl.pallas_call(functools.partial(reduce_kernel, count_z, count_y), in_spe...  9.36 us

profile of v2, /device:TPU:0, one launch (start us, length us, event | category | flops | bytes accessed | tf_op | source)
XLA Modules:
  0.0 240.5 jit_solution(13304905948866270459)
XLA Ops:
  0.0 0.6 pad_add_fusion.here_ref
  0.6 0.8 slice_subtract_fusion
  1.5 0.8 convert_reduce_fusion
  2.3 1.0 reshape.601
  3.5 2.5 %fusion.2.own_ref = f32[72,1024]{1,0:T(8,128)} fusion(s32[1024]{0:T(1024)S(1)} %convert_reduce_fusion, f32[3,1024]{1,0:T(4,128)S(1)} %add_convert_fusion, f32[64,1024]{1,0:T(8,128)S(1)} %reshape.602, f32[72]{0:T(128)S(1)} %pad.18.clone), kind=kOutput, calls=%fused_computation.5 | convolution fusion | flops 907165696 | bytes 573728 | tf_op jit(solution)/shard_map/dot_general | solution.py:349
  6.0 0.7 convert_element_type.53
  6.7 1.3 maximum_maximum_fusion.qm_ref
  8.1 54.7 %gather_atoms.1 = (f32[16,72,1024]{2,1,0:T(8,128)}, f32[32,8,128]{2,1,0:T(8,128)}) custom-call(f32[72,1024]{1,0:T(8,128)} %fusion.2.own_ref, f32[8,128]{1,0:T(8,128)} %maximum_maximum_fusion.qm_ref), custom_call_target="tpu_custom_call" | custom-call | tf_op jit(solution)/shard_map/gather_atoms/pallas_call | solution.py:461
  62.8 1.2 convert_reduce_fusion.1
  64.1 0.6 fusion.27
  64.9 0.6 and_select_fusion.count_ref
  65.5 76.0 %spread_lines.1.lines_ref = f32[2,2,8,648,128]{4,3,2,1,0:T(8,128)} custom-call(s32[1]{0:T(128)} %bitcast.kx_ref, s32[256]{0:T(256)} %copy-done.1, s32[256]{0:T(256)} %and_select_fusion.count_ref, f32[16,72,1024]{2,1,0:T(8,128)} %get-tuple-element.7.tab_ref, bf16[2,256,512]{2,1,0:T(8,128)(2,1)} %constant.152.clone.th_ref, ...), custom_call_target="tpu_custom_call" | custom-call | tf_op jit(solution)/shard_map/spread_lines/pallas_call | solution.py:584
  141.5 16.8 %swap_modes.1 = f32[2,2,8,648,128]{4,3,2,1,0:T(8,128)} custom-call(f32[2,2,8,648,128]{4,3,2,1,0:T(8,128)} %spread_lines.1.lines_ref), custom_call_target="tpu_custom_call" | custom-call | tf_op jit(solution)/shard_map/swap_modes/pallas_call | solution.py:628
  158.3 0.8 broadcast_in_dim.29.az_ref
  159.1 0.8 broadcast_in_dim.30.sz_ref
  160.0 0.7 multiply_multiply_fusion.6
  160.9 0.3 multiply_multiply_fusion.7
  161.3 3.3 %concatenate.41 = f32[32,16,256]{2,0,1:T(8,128)} concatenate(f32[3,16,256]{2,0,1:T(4,128)S(1)} %bitcast.18, f32[1,16,256]{2,0,1:T(1,128)S(1)} %get-tuple-element.35, f32[1,16,256]{2,0,1:T(1,128)S(1)} %get-tuple-element.40, f32[1,16,256]{2,0,1:T(1,128)S(1)} %get-tuple-element.38, f32[1,16,256]{2,0,1:T(1,128)S(1)} %get-tuple-element.39, f32[1,16,256]{2,0,1:T(1,128)S(1)} %get-tuple-element.41, ...), dimensions={0} | concatenate | bytes 1048576 | tf_op jit(solution)/shard_map/concatenate | solution.py:837
  164.5 1.2 broadcast_in_dim.33.step_ref
  165.7 62.7 %solve_interpolate.1 = f32[16,8,256]{2,1,0:T(8,128)} custom-call(s32[2]{0:T(128)} %pad_add_fusion.here_ref, f32[2,10368,128]{2,1,0:T(8,128)} %bitcast.14, bf16[384,432]{1,0:T(8,128)(2,1)} %constant.154.clone.fh_ref, bf16[384,432]{1,0:T(8,128)(2,1)} %constant.155.clone.fl_ref, bf16[392,384]{1,0:T(8,128)(2,1)} %constant.156.clone.bh_ref, ...), custom_call_target="tpu_custom_call" | custom-call | tf_op jit(solution)/shard_map/solve_interpolate/pallas_call | solution.py:754
  228.4 0.9 fusion.29
  229.2 0.6 pad_maximum_fusion
  229.9 9.4 %reduce_forces.1 = f32[8,128]{1,0:T(8,128)} custom-call(f32[32,8,128]{2,1,0:T(8,128)} %bitcast.17), custom_call_target="tpu_custom_call" | custom-call | tf_op jit(solution)/shard_map/reduce_forces/pallas_call | solution.py:797
  239.3 1.3 slice_multiply_fusion
  (29 shorter events, 0.9 us)
Async XLA Ops:
  64.8 0.7 copy-start.1
  141.5 19.3 %copy-start = (f32[32,8,128]{2,1,0:T(8,128)S(1)}, f32[32,8,128]{2,1,0:T(8,128)}, u32[]{:S(2)}) copy-start(f32[32,8,128]{2,1,0:T(8,128)} %get-tuple-element.8) | copy-start | bytes 393220
  141.5 23.1 %copy-start.2 = (f32[8,192]{1,0:T(8,128)S(1)}, f32[8,192]{1,0:T(8,128)}, u32[]{:S(2)}) copy-start(f32[8,192]{1,0:T(8,128)} %constant.163) | copy-start | bytes 18436
  165.7 73.6 %copy-start.3 = (f32[128]{0:T(128)S(1)}, f32[128]{0:T(128)}, u32[]{:S(2)}) copy-start(f32[128]{0:T(128)} %param.17) | copy-start | bytes 1540

commit v3 on v2

--- a/solution.py
+++ b/solution.py
@@ -349,6 +349,9 @@
     return jnp.dot(table, moves, precision=HIGHEST)
 
 
+PIECES = 3
+
+
 def gather_kernel(own_ref, qm_ref, tab_ref, all_ref, zs, zr, xs, xr, ys, yr, fs, fr, gs, gr, qm_send, qm_recv):
     p = lax.axis_index("gz")
     y = lax.axis_index("gy")
@@ -382,6 +385,25 @@
     near = ring + 1 - 2 * lax.rem(ring, 2)
     order = [ring, near, 1 + lower, (RING - 1) * lower]
 
+    def go(copies):
+        for c in copies:
+            c.start()
+
+    def pieces(src, dst, s, r, device):
+        size = tab_ref.shape[1] // PIECES
+        return [copy(src.at[pl.ds(k * size, size)], dst.at[pl.ds(k * size, size)], s, r, device) for k in range(PIECES)]
+
+    def along_parts(z, i):
+        src = own_ref if i == 0 else tab_ref.at[place(z, x, y)]
+        dst = tab_ref.at[place(z, x, y)]
+        return pieces(src, dst, zs.at[0, z], zr.at[z], above), pieces(src, dst, zs.at[1, z], zr.at[z], below)
+
+    def flat_parts(z, i):
+        src = own_ref if i == 0 else tab_ref.at[place(z, x, y)]
+        dst = tab_ref.at[place(z, x, y)]
+        both = zip(pieces(src, dst, xs.at[z], xr.at[z], aside), pieces(src, dst, ys.at[z], yr.at[z], over))
+        return [c for pair in both for c in pair]
+
     def along(z, i):
         src = own_ref if i == 0 else tab_ref.at[place(z, x, y)]
         dst = tab_ref.at[place(z, x, y)]
@@ -417,20 +439,20 @@
             c.start()
 
     for i, z in enumerate(order):
-        up, down = along(z, i)
         if i:
-            up.wait_recv()
+            along(z, i)[0].wait_recv()
+
+        ups, downs = along_parts(z, i)
 
         @pl.when(upward(z))
         def _():
-            up.start()
+            go(ups)
 
         @pl.when(downward(z))
         def _():
-            down.start()
-
-        for c in flat(z, i):
-            c.start()
+            go(downs)
+
+        go(flat_parts(z, i))
         if i:
             relay(order[i - 1])
     relay(order[-1])
@@ -476,17 +498,13 @@
 BLOCK = 256
 
 
-def lines_kernel(points, kx_local, z_used, kx_ref, first_ref, count_ref, tab_ref, th_ref, tl_ref, out_ref, grid_ref):
-    slab, half, block = pl.program_id(0), pl.program_id(1), pl.program_id(2)
-    blocks = pl.num_programs(2)
+def lines_kernel(points, kx_local, z_used, y_local, kx_ref, first_ref, count_ref, tab_ref, th_ref, tl_ref, out_ref, grid_ref):
+    slab = pl.program_id(0)
+    blocks = tab_ref.shape[2] // BLOCK
     modes = 2 * kx_local
     part = LANES // 2
     rows = ORDER * ORDER
-
-    @pl.when((half == 0) & (block == 0))
-    def _():
-        grid_ref[...] = jnp.zeros_like(grid_ref)
-
+    grid_ref[...] = jnp.zeros_like(grid_ref)
     lane = lax.broadcasted_iota(jnp.int32, (1, LANES), 1)
     mode = lax.broadcasted_iota(jnp.int32, (modes, LANES), 0)
     sine = mode >= kx_local
@@ -494,74 +512,93 @@
     shift = jnp.where(sine, points - points // 4, points).astype(F32)
     steps = [trig(kx * float(c), points) for c in range(ORDER)]
     wide = lax.broadcasted_iota(jnp.int32, (1, 2 * LANES), 1)
-    y_shift = wide // part
-    y_rows = lax.broadcasted_iota(jnp.int32, (2 * LANES, 2 * LANES), 0)
+    y_shift = (wide // part).astype(F32)
+    y_rows = lax.broadcasted_iota(jnp.int32, (2 * LANES, 2 * LANES), 0).astype(F32).astype(BF16)
     z_rows = lax.broadcasted_iota(jnp.int32, (8, 2 * LANES), 0)
-    base = ((slab * 2 + half) * blocks + block) * (BLOCK // part)
-    most = count_ref[base]
-    for g in range(1, BLOCK // part):
-        most = jnp.maximum(most, count_ref[base + g])
-
-    def step(it, carry):
-        for g in range(BLOCK // part):
-            tab = tab_ref[:, (g // 2) * LANES : (g // 2 + 1) * LANES]
-
-            def pair(even, odd):
-                if g % 2 == 0:
-                    return jnp.where(lane < part, even, pltpu.roll(odd, part, 1))
-                return jnp.where(lane < part, pltpu.roll(even, part, 1), odd)
-
-            weights = jnp.concatenate(
-                [pair(tab[0:rows], tab[rows : 2 * rows]), pair(tab[2 * rows : 3 * rows], tab[3 * rows : 4 * rows])], axis=1)
-            spots = tab[4 * rows : 4 * rows + 8]
-            spots = pair(spots, spots)
-            twice = jnp.concatenate([spots, spots], axis=1).astype(jnp.int32)
-            z_first = first_ref[base + g] + it * Z_STEP
-            live = it < count_ref[base + g]
-            off = z_rows + jnp.where(live, z_first, 4 * points) - twice[0:1]
-            z_first = jnp.minimum(z_first, z_used - 1)
-            cosine, sinus = trig(kx * spots[2:3] + shift, points)
-            waves, picks = [], []
-            for c in range(ORDER):
-                wave = cosine * steps[c][0] - sinus * steps[c][1] if c else cosine
-                waves.append(jnp.concatenate([wave, wave], axis=1))
-                pick = jnp.zeros((8, 2 * LANES), F32)
-                for a in range(ORDER):
-                    pick = jnp.where(off == a, weights[a * ORDER + c : a * ORDER + c + 1], pick)
-                picks.append(pick)
-            pieces = []
-            for z in range(Z_STEP):
-                value = picks[0][z : z + 1] * waves[0]
-                for c in range(1, ORDER):
-                    value += picks[c][z : z + 1] * waves[c]
-                pieces.append(value)
-            high, low = split(jnp.concatenate(pieces, axis=0))
-            hits = jnp.where(y_rows == twice[1:2] + y_shift, 1.0, 0.0).astype(BF16)
-            across = (((1,), (1,)), ((), ()))
-            total = lax.dot_general(high, hits, across, preferred_element_type=F32)
-            total += lax.dot_general(low, hits, across, preferred_element_type=F32)
-            grid_ref[half, pl.ds(pl.multiple_of(z_first * modes, 8), Z_STEP * modes), :] += total
+    across = (((1,), (1,)), ((), ()))
+
+    def some(i, outer):
+        half = i // blocks
+        at = lax.rem(i, blocks)
+        sign = (1 - 2 * half).astype(F32)
+        start = (ORDER - 1 + half * (y_local - 1)).astype(F32)
+        base = (slab * 2 * blocks + i) * (BLOCK // part)
+        most = count_ref[base]
+        for g in range(1, BLOCK // part):
+            most = jnp.maximum(most, count_ref[base + g])
+
+        def step(it, carry):
+            for t in range(BLOCK // LANES):
+                tab = tab_ref[half, :, pl.ds(pl.multiple_of(at * BLOCK + t * LANES, LANES), LANES)]
+                spots = tab[4 * rows : 4 * rows + 8]
+                cosine, sinus = trig(kx * spots[2:3] + shift, points)
+                waves = [cosine] + [cosine * steps[c][0] - sinus * steps[c][1] for c in range(1, ORDER)]
+                rolled = [pltpu.roll(wave, part, 1) for wave in waves]
+                turned = pltpu.roll(tab, part, 1)
+                for h in range(2):
+                    group = base + 2 * t + h
+
+                    def pair(even, odd, even_turned, odd_turned):
+                        if h == 0:
+                            return jnp.where(lane < part, even, odd_turned)
+                        return jnp.where(lane < part, even_turned, odd)
+
+                    def cut(b):
+                        return tab[b * rows : (b + 1) * rows], turned[b * rows : (b + 1) * rows]
+
+                    def pick_pair(b):
+                        even, even_turned = cut(b)
+                        odd, odd_turned = cut(b + 1)
+                        return pair(even, odd, even_turned, odd_turned)
+
+                    weights = jnp.concatenate([pick_pair(0), pick_pair(2)], axis=1)
+                    turned_spots = turned[4 * rows : 4 * rows + 8]
+                    here = pair(spots, spots, turned_spots, turned_spots)
+                    here = jnp.concatenate([here, here], axis=1)
+                    z_first = first_ref[group] + it * Z_STEP
+                    live = it < count_ref[group]
+                    off = z_rows + jnp.where(live, z_first, 4 * points) - here[0:1].astype(jnp.int32)
+                    z_first = jnp.minimum(z_first, z_used - 1)
+                    picks = []
+                    for c in range(ORDER):
+                        pick = jnp.zeros((8, 2 * LANES), F32)
+                        for a in range(ORDER):
+                            pick = jnp.where(off == a, weights[a * ORDER + c : a * ORDER + c + 1], pick)
+                        picks.append(pick)
+                    own = [pair(wave, wave, back, back) for wave, back in zip(waves, rolled)]
+                    own = [jnp.concatenate([wave, wave], axis=1) for wave in own]
+                    pieces = []
+                    for z in range(Z_STEP):
+                        value = picks[0][z : z + 1] * own[0]
+                        for c in range(1, ORDER):
+                            value += picks[c][z : z + 1] * own[c]
+                        pieces.append(value)
+                    high, low = split(jnp.concatenate(pieces, axis=0))
+                    y_cell = (start + sign * (here[1:2] + y_shift)).astype(BF16)
+                    hits = jnp.where(y_rows == y_cell, jnp.ones((), BF16), jnp.zeros((), BF16))
+                    total = lax.dot_general(high, hits, across, preferred_element_type=F32)
+                    total += lax.dot_general(low, hits, across, preferred_element_type=F32)
+                    grid_ref[half, pl.ds(pl.multiple_of(z_first * modes, 8), Z_STEP * modes), :] += total
+            return carry
+
+        lax.fori_loop(0, most, step, 0)
+        return outer
+
+    lax.fori_loop(0, 2 * blocks, some, 0)
+    cuts = 3
+    size = z_used * modes // cuts
+
+    def chunk(i, carry):
+        at = pl.multiple_of(i * size, 8)
+        one, two = grid_ref[0, pl.ds(at, size), :], grid_ref[1, pl.ds(at, size), :]
+        for k, value in enumerate((one + two, one - two)):
+            high, low = split(value)
+            found = dot3(high, low, th_ref[k], tl_ref[k])
+            for t in range(2):
+                out_ref[k, t, pl.ds(at, size), :] = found[:, t * LANES : (t + 1) * LANES]
         return carry
 
-    lax.fori_loop(0, most, step, 0)
-
-    @pl.when((half == 1) & (block == blocks - 1))
-    def _():
-        cuts = 3
-        size = z_used * modes // cuts
-
-        def chunk(i, carry):
-            at = pl.multiple_of(i * size, 8)
-            total = None
-            for h in range(2):
-                high, low = split(grid_ref[h, pl.ds(at, size), :])
-                found = dot3(high, low, th_ref[h], tl_ref[h])
-                total = found if total is None else total + found
-            for t in range(4):
-                out_ref[t // 2, t % 2, pl.ds(at, size), :] = total[:, t * LANES : (t + 1) * LANES]
-            return carry
-
-        lax.fori_loop(0, cuts, chunk, 0)
+    lax.fori_loop(0, cuts, chunk, 0)
 
 
 def spread(tab, kx_first, kx_local, z_local, y_local, points):
@@ -574,30 +611,30 @@
     first = jnp.min(z_cell, axis=-1)
     counts = (jnp.max(z_cell, axis=-1) - first + ORDER + Z_STEP - 1) // Z_STEP
     k = np.arange(points // 2)
-    cell = (np.arange(2)[:, None] * y_local + np.arange(2 * LANES)[None, :]) % points
-    angle = 2.0 * np.pi / points * ((cell[:, :, None] * k) % points)
-    table = np.zeros((2, 2 * LANES, 2, 2 * LANES))
-    table[:, :, 0, : points // 2] = np.cos(angle)
-    table[:, :, 1, : points // 2] = np.sin(angle)
-    th, tl = split_table(table.reshape(2, 2 * LANES, 4 * LANES))
-    whole = lambda s, h, b, *_: (0, 0, 0)
+    cell = 2 * (np.arange(2 * LANES) - (ORDER - 1)) + 1
+    angle = np.pi / points * ((cell[:, None] * k) % (2 * points))
+    table = np.zeros((2, 2 * LANES, 2 * LANES))
+    table[0, :, : points // 2] = np.cos(angle)
+    table[1, :, : points // 2] = np.sin(angle)
+    th, tl = split_table(table)
+    whole = lambda s, *_: (0, 0, 0)
     return pl.pallas_call(
-        functools.partial(lines_kernel, points, kx_local, z_used),
+        functools.partial(lines_kernel, points, kx_local, z_used, y_local),
         grid_spec=pltpu.PrefetchScalarGridSpec(
             num_scalar_prefetch=3,
-            grid=(slabs, 2, count // BLOCK),
+            grid=(slabs,),
             in_specs=[
-                pl.BlockSpec((None, rows, BLOCK), lambda s, h, b, *_: (s * 2 + h, 0, b)),
+                pl.BlockSpec((None, 2, rows, count), lambda s, *_: (s, 0, 0, 0)),
                 pl.BlockSpec(th.shape, whole),
                 pl.BlockSpec(tl.shape, whole),
             ],
-            out_specs=pl.BlockSpec((2, 2, None, z_used * modes, LANES), lambda s, h, b, *_: (0, 0, s, 0, 0)),
+            out_specs=pl.BlockSpec((2, 2, None, z_used * modes, LANES), lambda s, *_: (0, 0, s, 0, 0)),
             scratch_shapes=[pltpu.VMEM((2, (z_used + Z_STEP - 1) * modes, 2 * LANES), F32)],
         ),
         out_shape=jax.ShapeDtypeStruct((2, 2, slabs, z_used * modes, LANES), F32),
-        compiler_params=pltpu.CompilerParams(dimension_semantics=("arbitrary",) * 3, vmem_limit_bytes=VMEM_LIMIT),
+        compiler_params=pltpu.CompilerParams(dimension_semantics=("arbitrary",), vmem_limit_bytes=VMEM_LIMIT),
         name="spread_lines",
-    )(kx_first.reshape(1), first.reshape(-1), counts.reshape(-1), tab, th, tl)
+    )(kx_first.reshape(1), first.reshape(-1), counts.reshape(-1), tab.reshape(slabs, 2, rows, count), th, tl)
 
 
 def swap_kernel(lines_ref, out_ref, send_sem, recv_sem):
@@ -608,57 +645,74 @@
     barrier = pltpu.get_barrier_semaphore()
     pl.semaphore_signal(barrier, inc=1, device_id=(other, y), device_id_type=MESH)
     pl.semaphore_wait(barrier, 1)
-    copy = pltpu.make_async_remote_copy(
-        src_ref=lines_ref.at[1 - core], dst_ref=out_ref.at[:, core], send_sem=send_sem, recv_sem=recv_sem,
-        device_id=(other, y), device_id_type=MESH)
-    copy.start()
-
-    def keep(i, carry):
-        for t in range(2):
-            out_ref[t, core, i] = lines_ref[core, t, i]
-        return carry
-
-    lax.fori_loop(0, lines_ref.shape[2], keep, 0)
-    copy.wait()
+    copies = []
+    for t in range(out_ref.shape[0]):
+        for i in range(out_ref.shape[1]):
+            copies.append(pltpu.make_async_remote_copy(
+                src_ref=lines_ref.at[1 - core, t, i], dst_ref=out_ref.at[t, i], send_sem=send_sem.at[t, i],
+                recv_sem=recv_sem.at[t, i], device_id=(other, y), device_id_type=MESH))
+            copies[-1].start()
+    for copy in copies:
+        copy.wait()
 
 
 def swap(lines):
     types, tiles, slabs, deep, lanes = lines.shape
-    vmem = pl.BlockSpec(memory_space=pltpu.VMEM)
-    out = pl.pallas_call(
+    space = pl.BlockSpec(memory_space=pl.ANY)
+    return pl.pallas_call(
         swap_kernel,
-        in_specs=[vmem],
-        out_specs=vmem,
-        out_shape=jax.ShapeDtypeStruct((tiles, 2, slabs, deep, lanes), F32),
-        scratch_shapes=[pltpu.SemaphoreType.DMA, pltpu.SemaphoreType.DMA],
+        in_specs=[space],
+        out_specs=space,
+        out_shape=jax.ShapeDtypeStruct((tiles, slabs, deep, lanes), F32),
+        scratch_shapes=[pltpu.SemaphoreType.DMA((tiles, slabs)), pltpu.SemaphoreType.DMA((tiles, slabs))],
         compiler_params=pltpu.CompilerParams(collective_id=1, has_side_effects=True, vmem_limit_bytes=VMEM_LIMIT),
         name="swap_modes",
     )(lines)
-    return out.reshape(tiles, 2 * slabs * deep, lanes)
-
-
-def solve_kernel(points, kx_local, here_ref, x_ref, fh_ref, fl_ref, bh_ref, bl_ref, az_ref, sz_ref, col_ref, sq_ref, step_ref, qm_ref, out_ref, pot_ref, wave_h, wave_l, wx_ref, acc_ref):
+
+
+PACK = 4
+
+
+def solve_kernel(points, kx_local, here_ref, x_ref, y_ref, fh_ref, fl_ref, bh_ref, bl_ref, az_ref, sz_ref, col_ref, sq_ref, qm_ref, out_ref, pot_ref, wave_h, wave_l, wx_ref, acc_ref, step_ref):
     modes = 2 * kx_local
-    deep = x_ref.shape[1] // modes
+    deep = y_ref.shape[1] // modes
     half = points // 2
-    slabs = qm_ref.shape[0]
+    slabs = qm_ref.shape[0] // 2
     z_local = points // slabs
-    atoms = qm_ref.shape[2]
-    kx_first, y_shift = here_ref[0], here_ref[1]
-
-    def convolve(m, carry):
-        data = jnp.concatenate([x_ref[t, pl.ds(m, deep, stride=modes), :] for t in range(2)], axis=1)
-        high, low = split(data)
-        coef = dot3(fh_ref[...], fl_ref[...], high, low)
-        total = sz_ref[...] + sq_ref[pl.ds(m, 1), :]
+    atoms = 2 * qm_ref.shape[2]
+    kx_first, core = here_ref[0], here_ref[1]
+    y_shift = 2 * points - core * (points // 2)
+
+    lane = lax.broadcasted_iota(jnp.int32, (1, LANES), 1)
+    part = half - LANES
+    wide = PACK * half // LANES
+    for c in range(ORDER):
+        ky_lane = lax.broadcasted_iota(jnp.int32, (half, LANES), 0).astype(F32)
+        step_ref[c], step_ref[ORDER + c] = trig(ky_lane * float(c), points)
+
+    def convolve(i, carry):
+        def column(m, t):
+            return jnp.concatenate(
+                [x_ref[core, t, pl.ds(m, deep, stride=modes), :], y_ref[t, pl.ds(m, deep, stride=modes), :]], axis=0)
+
+        heads = [column(PACK * i + j, 0) for j in range(PACK)]
+        tails = [column(PACK * i + j, 1) for j in range(PACK)]
+        tails = [jnp.where(lane < part, tails[j], pltpu.roll(tails[j + 1], part, 1)) for j in range(0, PACK, 2)]
+        high, low = split(jnp.concatenate(heads + tails, axis=1))
+        coef = dot3(fh_ref[core], fl_ref[core], high, low)
+        total = jnp.concatenate([sz_ref[...]] * wide, axis=1) + sq_ref[pl.ds(i, 1), :]
         keep = total > 0.0
-        value = az_ref[...] * col_ref[pl.ds(m, 1), :] / jnp.where(keep, total, 1.0)
+        value = jnp.concatenate([az_ref[...]] * wide, axis=1) * col_ref[pl.ds(i, 1), :] / jnp.where(keep, total, 1.0)
         green = jnp.where(keep, value, 0.0)
         high, low = split(coef * jnp.concatenate([green, green], axis=0))
-        pot_ref[m] = dot3(bh_ref[...], bl_ref[...], high, low)
+        back = dot3(bh_ref[...], bl_ref[...], high, low)
+        for j in range(PACK):
+            pot_ref[PACK * i + j, :, :LANES] = back[:, j * LANES : (j + 1) * LANES]
+            tail = back[:, (PACK + j // 2) * LANES : (PACK + j // 2 + 1) * LANES]
+            pot_ref[PACK * i + j, :, LANES:] = pltpu.roll(tail, LANES - part, 1) if j % 2 else tail
         return carry
 
-    lax.fori_loop(0, modes, convolve, 0)
+    lax.fori_loop(0, modes // PACK, convolve, 0)
     span = 4 * 8
     wave_h[half:] = jnp.zeros((2 * LANES - half, 2 * atoms), BF16)
     wave_l[half:] = jnp.zeros((2 * LANES - half, 2 * atoms), BF16)
@@ -669,9 +723,14 @@
     x_shift = jnp.where(sine, points - points // 4, points).astype(F32)
 
     def slab(p, carry):
-        qm = qm_ref[p]
-        row = lambda i: qm[i : i + 1]
-        cosine, sinus = trig(ky * row(1) + y_shift.astype(F32), points)
+        qm = jnp.concatenate([qm_ref[2 * p], qm_ref[2 * p + 1]], axis=1)
+        values, slopes = spline_rows(qm)
+        table = [qm[0:1], qm[1:2], qm[2:3]]
+        for d in range(3, 6):
+            for part in (values, slopes):
+                table += [v[d : d + 1] for v in part]
+        row = lambda i: table[i]
+        cosine, sinus = trig(ky * (2.0 * row(1) + 1.0) + y_shift.astype(F32), 2 * points)
         for k, at in ((0, 11), (1, 15)):
             real = imag = None
             for c in range(ORDER):
@@ -708,19 +767,40 @@
             wz = jnp.where(off == a, row(3 + a), wz)
             dz = jnp.where(off == a, row(7 + a), dz)
         total = lambda v: jnp.sum(v, axis=0, keepdims=True)
-        out_ref[p] = jnp.concatenate(
+        found = jnp.concatenate(
             [total(acc_ref[0] * dz), total(acc_ref[1] * wz), total(acc_ref[2] * wz), jnp.zeros((5, atoms), F32)], axis=0)
+        out_ref[2 * p] = found[:, : atoms // 2]
+        out_ref[2 * p + 1] = found[:, atoms // 2 :]
         return carry
 
     lax.fori_loop(0, slabs, slab, 0)
 
 
-def solve(lines, here, qm_table, kx_index, points):
-    tiles, deep, lanes = lines.shape
+def spline_rows(frac):
+    remain = 1.0 - frac
+    square = frac * frac
+    cubed = square * frac
+    values = [
+        remain * remain * remain / 6.0,
+        (3.0 * cubed - 6.0 * square + 4.0) / 6.0,
+        (-3.0 * cubed + 3.0 * square + 3.0 * frac + 1.0) / 6.0,
+        cubed / 6.0,
+    ]
+    slopes = [
+        -0.5 * remain * remain,
+        (3.0 * square - 4.0 * frac) / 2.0,
+        (-3.0 * square + 2.0 * frac + 1.0) / 2.0,
+        0.5 * square,
+    ]
+    return values, slopes
+
+
+def solve(lines, other, here, qm_all, kx_index, points):
+    tiles, slab_half, deep, lanes = other.shape
     kx_local = kx_index.shape[0]
     modes = 2 * kx_local
     half = points // 2
-    slabs, _, atoms = qm_table.shape
+    slabs, atoms = qm_all.shape[0] // 2, 2 * qm_all.shape[2]
     z_local = points // slabs
     z_used = z_local + ORDER - 1
     k = np.arange(half)
@@ -730,7 +810,8 @@
         return np.concatenate([np.cos(angle), np.sin(angle)], axis=0)
 
     core, pair, plane = np.meshgrid(np.arange(2), np.arange(slabs // 2), np.arange(z_used), indexing="ij")
-    fh, fl = split_table(waves((((pair * 2 + core) * z_local + plane) % points).reshape(-1)))
+    cells = (((pair * 2 + core) * z_local + plane) % points).reshape(2, -1)
+    fh, fl = split_table(np.stack([waves(cells.reshape(-1)), waves(cells[::-1].reshape(-1))]))
     reach = points + 8
     bh, bl = split_table(waves(np.arange(reach) % points).T)
 
@@ -741,31 +822,33 @@
 
     z_sq, z_fac = parts_of(jnp.asarray(k, jnp.int32))
     x_sq, x_fac = parts_of(jnp.concatenate([kx_index, kx_index]))
-    pad = (0, 2 * lanes - half)
-    y_sq, y_fac = jnp.pad(z_sq, pad), jnp.pad(z_fac, pad)
-    col = x_fac[:, None] * y_fac[None, :] * (1.0 / (math.pi * float(points) ** 3))
-    sq = x_sq[:, None] + y_sq[None, :]
-    az = jnp.broadcast_to(z_fac[:, None], (half, 2 * lanes))
-    sz = jnp.broadcast_to(z_sq[:, None], (half, 2 * lanes))
-    turn = 2.0 * np.pi / points * (np.arange(ORDER)[:, None] * k[None, :] % points)
-    step = np.concatenate([np.cos(turn), np.sin(turn)], axis=0)
-    step = jnp.broadcast_to(jnp.asarray(step[:, :, None], F32), step.shape + (lanes,))
+
+    def packed(table):
+        table = table.reshape(modes // PACK, PACK, half)
+        head = table[:, :, :lanes].reshape(modes // PACK, PACK * lanes)
+        return jnp.concatenate([head, table[:, :, lanes:].reshape(modes // PACK, -1)], axis=1)
+
+    col = packed(x_fac[:, None] * z_fac[None, :] * (1.0 / (math.pi * float(points) ** 3)))
+    sq = packed(x_sq[:, None] + z_sq[None, :])
+    az = jnp.broadcast_to(z_fac[:, None], (half, lanes))
+    sz = jnp.broadcast_to(z_sq[:, None], (half, lanes))
     vmem = pl.BlockSpec(memory_space=pltpu.VMEM)
     return pl.pallas_call(
         functools.partial(solve_kernel, points, kx_local),
         in_specs=[pl.BlockSpec(memory_space=pltpu.SMEM)] + [vmem] * 11,
         out_specs=vmem,
-        out_shape=jax.ShapeDtypeStruct((slabs, 8, atoms), F32),
+        out_shape=jax.ShapeDtypeStruct((2 * slabs, 8, atoms // 2), F32),
         scratch_shapes=[
             pltpu.VMEM((modes, reach, 2 * lanes), F32),
             pltpu.VMEM((2 * lanes, 2 * atoms), BF16),
             pltpu.VMEM((2 * lanes, 2 * atoms), BF16),
             pltpu.VMEM((2, modes, atoms), F32),
             pltpu.VMEM((3, 32, atoms), F32),
+            pltpu.VMEM((2 * ORDER, half, lanes), F32),
         ],
         compiler_params=pltpu.CompilerParams(vmem_limit_bytes=VMEM_LIMIT),
         name="solve_interpolate",
-    )(here, lines, fh, fl, bh, bl, az, sz, col, sq, step, qm_table)
+    )(here, lines.reshape(2, tiles, slab_half * deep, lanes), other.reshape(tiles, slab_half * deep, lanes), fh, fl, bh, bl, az, sz, col, sq, qm_all)
 
 
 def reduce_kernel(count_z, count_y, part_ref, out_ref, land_ref, send_sem, recv_sem):
@@ -828,19 +911,9 @@
 
     kx_first = ((p // 2) * count_y + q) * kx_local
     lines = spread(tab, kx_first, kx_local, z_local, y_local, points)
-    lines = swap(lines)
-
-    qm_all = qm_all.transpose(1, 0, 2).reshape(8, count_z, count_y * qm_count)
-    w_z, d_z = spline_weights(qm_all[3])
-    w_y, d_y = spline_weights(qm_all[4])
-    w_x, d_x = spline_weights(qm_all[5])
-    qm_table = jnp.concatenate([qm_all[:3], w_z, d_z, w_y, d_y, w_x, d_x, jnp.zeros((5,) + qm_all.shape[1:], F32)], axis=0)
-    qm_table = qm_table.transpose(1, 0, 2)
+    other = swap(lines)
     kx_index = kx_first + jnp.arange(kx_local, dtype=jnp.int32)
-    y_shift = jnp.where(p % 2 == 0, points, points - points // 4)
-    here = jnp.stack([kx_first, y_shift])
-    partial = solve(lines, here, qm_table, kx_index, points)
-    partial = partial.reshape(count_z, 8, count_y, qm_count).transpose(0, 2, 1, 3).reshape(count_z * count_y, 8, qm_count)
+    partial = solve(lines, other, jnp.stack([kx_first, p % 2]), qm_all, kx_index, points)
     forces = reduce_forces(partial, count_z, count_y)
     return -qm_charge * forces[:3]
 

time: 242 us -> 191 us (0.79)
  Pallas kernels: 220 us -> 175 us
  local copies, waits for them, and re-layouts: 8.45 us -> 3.24 us
    pallas_call x2, Pallas kernels: 92.8 us -> 63.3 us  [the longest x1 54 us: spread(): pl.pallas_call(functools.partial(lines_kernel, points, kx_local, z_used,...]
    pallas_call x1, Pallas kernels: 62.7 us -> 47.6 us  [solve(): pl.pallas_call(functools.partial(solve_kernel, points, kx_local), in_spec...]
    concatenate x1, local copies, waits for them, and re-layouts: 3.26 us -> 0.08 us  [solve(): x_sq, x_fac = parts_of(jnp.concatenate([kx_index, kx_index]))]
where the time goes in v3:
time: 191 us; the launch traced here: 190 us
  Pallas kernels  175 us (92%)
  other arithmetic  9.39 us (5%)
  local copies, waits for them, and re-layouts  3.24 us (2%)
  matrix products  2.45 us (1%)
    pallas_call x1, Pallas kernels, gather(): pl.pallas_call(gather_kernel, out_shape=(jax.ShapeDtypeStruct((RING * 4,)...  54.8 us
    pallas_call x1, Pallas kernels, spread(): pl.pallas_call(functools.partial(lines_kernel, points, kx_local, z_used,...  54 us
    pallas_call x1, Pallas kernels, solve(): pl.pallas_call(functools.partial(solve_kernel, points, kx_local), in_spec...  47.6 us
    pallas_call x1, Pallas kernels, swap(): pl.pallas_call(swap_kernel, in_specs=[space], out_specs=space, out_shape=...  9.38 us
    pallas_call x1, Pallas kernels, reduce_forces(): pl.pallas_call(functools.partial(reduce_kernel, count_z, count_y), in_spe...  9.36 us

profile of v3, /device:TPU:0, one launch (start us, length us, event | category | flops | bytes accessed | tf_op | source)
XLA Modules:
  0.0 190.4 jit_solution(12805512437183882692)
XLA Ops:
  0.0 0.8 slice_subtract_fusion
  0.9 0.8 convert_reduce_fusion
  1.6 1.0 reshape.134
  2.7 0.1 reshape.135
  2.9 2.5 %fusion.2.own_ref = f32[72,1024]{1,0:T(8,128)} fusion(s32[1024]{0:T(1024)S(1)} %convert_reduce_fusion, f32[3,1024]{1,0:T(4,128)S(1)} %add_convert_fusion, f32[64,1024]{1,0:T(8,128)S(1)} %reshape.135, f32[72]{0:T(128)S(1)} %pad.11.clone), kind=kOutput, calls=%fused_computation.5 | convolution fusion | flops 907165696 | bytes 573728 | tf_op jit(solution)/shard_map/dot_general | solution.py:349
  5.3 0.7 convert_element_type.50
  6.1 1.3 maximum_maximum_fusion.qm_ref
  7.4 54.8 %gather_atoms.1 = (f32[16,72,1024]{2,1,0:T(8,128)}, f32[32,8,128]{2,1,0:T(8,128)}) custom-call(f32[72,1024]{1,0:T(8,128)} %fusion.2.own_ref, f32[8,128]{1,0:T(8,128)} %maximum_maximum_fusion.qm_ref), custom_call_target="tpu_custom_call" | custom-call | tf_op jit(solution)/shard_map/gather_atoms/pallas_call | solution.py:483
  62.2 1.2 convert_reduce_fusion.1
  63.5 0.1 convert_element_type.52
  63.5 0.6 fusion.23
  64.3 0.6 and_select_fusion.count_ref
  64.9 54.0 %spread_lines.1.lines_ref = f32[2,2,8,648,128]{4,3,2,1,0:T(8,128)} custom-call(s32[1]{0:T(128)} %bitcast.kx_ref, s32[256]{0:T(256)} %copy-done, s32[256]{0:T(256)} %and_select_fusion.count_ref, f32[8,2,72,1024]{3,2,1,0:T(8,128)} %bitcast.21, bf16[2,256,256]{2,1,0:T(8,128)(2,1)} %constant.111.clone.th_ref, bf16[2,256,256]{2,1,0:T(8,128)(2,1)} %constant.112.clone.tl_ref), custom_call_target="tpu_custom_call" | custom-call | tf_op jit(solution)/shard_map/spread_lines/pallas_call | solution.py:621
  118.8 9.4 %swap_modes.1 = f32[2,8,648,128]{3,2,1,0:T(8,128)} custom-call(f32[2,2,8,648,128]{4,3,2,1,0:T(8,128)} %spread_lines.1.lines_ref), custom_call_target="tpu_custom_call" | custom-call | tf_op jit(solution)/shard_map/swap_modes/pallas_call | solution.py:662
  128.2 0.1 add_reduce_fusion
  128.7 0.6 pad_maximum_fusion.col_ref
  129.4 0.1 reshape.143
  129.4 0.6 pad_maximum_fusion.1.sq_ref
  130.1 0.6 pad_add_fusion.here_ref
  130.7 0.7 broadcast_in_dim.23.az_ref
  131.4 0.7 broadcast_in_dim.24.sz_ref
  132.1 47.6 %solve_interpolate.1.part_ref = f32[32,8,128]{2,1,0:T(8,128)} custom-call(s32[2]{0:T(128)} %pad_add_fusion.here_ref, f32[2,2,5184,128]{3,2,1,0:T(8,128)} %bitcast.19, f32[2,5184,128]{2,1,0:T(8,128)} %bitcast.20, bf16[2,384,432]{2,1,0:T(8,128)(2,1)} %constant.113.clone.fh_ref, bf16[2,384,432]{2,1,0:T(8,128)(2,1)} %constant.114.clone.fl_ref, ...), custom_call_target="tpu_custom_call" | custom-call | tf_op jit(solution)/shard_map/solve_interpolate/pallas_call | solution.py:836
  179.7 9.4 %reduce_forces.1 = f32[8,128]{1,0:T(8,128)} custom-call(f32[32,8,128]{2,1,0:T(8,128)} %solve_interpolate.1.part_ref), custom_call_target="tpu_custom_call" | custom-call | tf_op jit(solution)/shard_map/reduce_forces/pallas_call | solution.py:880
  189.1 1.3 slice_multiply_fusion
  (26 shorter events, 0.7 us)
Async XLA Ops:
  64.2 0.6 copy-start
  132.1 57.0 %copy-start.1 = (f32[128]{0:T(128)S(1)}, f32[128]{0:T(128)}, u32[]{:S(2)}) copy-start(f32[128]{0:T(128)} %param.16) | copy-start | bytes 1540

commit v4 on v3

--- a/solution.py
+++ b/solution.py
@@ -495,7 +495,7 @@
 
 
 Z_STEP = 6
-BLOCK = 256
+BLOCK = 512
 
 
 def lines_kernel(points, kx_local, z_used, y_local, kx_ref, first_ref, count_ref, tab_ref, th_ref, tl_ref, out_ref, grid_ref):
@@ -670,7 +670,7 @@
     )(lines)
 
 
-PACK = 4
+PACK = 8
 
 
 def solve_kernel(points, kx_local, here_ref, x_ref, y_ref, fh_ref, fl_ref, bh_ref, bl_ref, az_ref, sz_ref, col_ref, sq_ref, qm_ref, out_ref, pot_ref, wave_h, wave_l, wx_ref, acc_ref, step_ref):

time: 191 us -> 179 us (0.937)
  Pallas kernels: 175 us -> 164 us
    pallas_call x1, Pallas kernels: 47.6 us -> 41.7 us  [solve(): pl.pallas_call(functools.partial(solve_kernel, points, kx_local), in_spec...]
    pallas_call x1, Pallas kernels: 54 us -> 48.3 us  [spread(): pl.pallas_call(functools.partial(lines_kernel, points, kx_local, z_used,...]
where the time goes in v4:
time: 179 us
  Pallas kernels  164 us (92%)
  other arithmetic  9.38 us (5%)
  local copies, waits for them, and re-layouts  3.25 us (2%)
  matrix products  2.45 us (1%)
    pallas_call x1, Pallas kernels, gather(): pl.pallas_call(gather_kernel, out_shape=(jax.ShapeDtypeStruct((RING * 4,)...  54.8 us
    pallas_call x1, Pallas kernels, spread(): pl.pallas_call(functools.partial(lines_kernel, points, kx_local, z_used,...  48.3 us
    pallas_call x1, Pallas kernels, solve(): pl.pallas_call(functools.partial(solve_kernel, points, kx_local), in_spec...  41.7 us
    pallas_call x1, Pallas kernels, swap(): pl.pallas_call(swap_kernel, in_specs=[space], out_specs=space, out_shape=...  9.38 us
    pallas_call x1, Pallas kernels, reduce_forces(): pl.pallas_call(functools.partial(reduce_kernel, count_z, count_y), in_spe...  9.36 us

profile of v4, /device:TPU:0, one launch (start us, length us, event | category | flops | bytes accessed | tf_op | source)
XLA Modules:
  0.0 178.8 jit_solution(12762601466721279873)
XLA Ops:
  0.0 0.8 slice_subtract_fusion
  0.9 0.8 convert_reduce_fusion
  1.6 1.0 reshape.134
  2.7 0.1 reshape.135
  2.9 2.5 %fusion.2.own_ref = f32[72,1024]{1,0:T(8,128)} fusion(s32[1024]{0:T(1024)S(1)} %convert_reduce_fusion, f32[3,1024]{1,0:T(4,128)S(1)} %add_convert_fusion, f32[64,1024]{1,0:T(8,128)S(1)} %reshape.135, f32[72]{0:T(128)S(1)} %pad.11.clone), kind=kOutput, calls=%fused_computation.5 | convolution fusion | flops 907165696 | bytes 573728 | tf_op jit(solution)/shard_map/dot_general | solution.py:349
  5.3 0.7 convert_element_type.50
  6.1 1.3 maximum_maximum_fusion.qm_ref
  7.4 54.8 %gather_atoms.1 = (f32[16,72,1024]{2,1,0:T(8,128)}, f32[32,8,128]{2,1,0:T(8,128)}) custom-call(f32[72,1024]{1,0:T(8,128)} %fusion.2.own_ref, f32[8,128]{1,0:T(8,128)} %maximum_maximum_fusion.qm_ref), custom_call_target="tpu_custom_call" | custom-call | tf_op jit(solution)/shard_map/gather_atoms/pallas_call | solution.py:483
  62.2 1.2 convert_reduce_fusion.1
  63.4 0.1 convert_element_type.52
  63.5 0.6 fusion.24
  64.3 0.6 and_select_fusion.count_ref
  64.9 48.3 %spread_lines.1.lines_ref = f32[2,2,8,648,128]{4,3,2,1,0:T(8,128)} custom-call(s32[1]{0:T(128)} %bitcast.kx_ref, s32[256]{0:T(256)} %copy-done, s32[256]{0:T(256)} %and_select_fusion.count_ref, f32[8,2,72,1024]{3,2,1,0:T(8,128)} %bitcast.21, bf16[2,256,256]{2,1,0:T(8,128)(2,1)} %constant.111.clone.th_ref, bf16[2,256,256]{2,1,0:T(8,128)(2,1)} %constant.112.clone.tl_ref), custom_call_target="tpu_custom_call" | custom-call | tf_op jit(solution)/shard_map/spread_lines/pallas_call | solution.py:621
  113.1 9.4 %swap_modes.1 = f32[2,8,648,128]{3,2,1,0:T(8,128)} custom-call(f32[2,2,8,648,128]{4,3,2,1,0:T(8,128)} %spread_lines.1.lines_ref), custom_call_target="tpu_custom_call" | custom-call | tf_op jit(solution)/shard_map/swap_modes/pallas_call | solution.py:662
  122.5 0.1 add_reduce_fusion
  122.6 0.1 concatenate.35
  123.0 0.6 pad_maximum_fusion.col_ref
  123.7 0.6 pad_maximum_fusion.1.sq_ref
  124.3 0.6 pad_add_fusion.here_ref
  124.9 0.7 broadcast_in_dim.23.az_ref
  125.7 0.7 broadcast_in_dim.24.sz_ref
  126.4 41.7 %solve_interpolate.1.part_ref = f32[32,8,128]{2,1,0:T(8,128)} custom-call(s32[2]{0:T(128)} %pad_add_fusion.here_ref, f32[2,2,5184,128]{3,2,1,0:T(8,128)} %bitcast.19, f32[2,5184,128]{2,1,0:T(8,128)} %bitcast.20, bf16[2,384,432]{2,1,0:T(8,128)(2,1)} %constant.113.clone.fh_ref, bf16[2,384,432]{2,1,0:T(8,128)(2,1)} %constant.114.clone.fl_ref, ...), custom_call_target="tpu_custom_call" | custom-call | tf_op jit(solution)/shard_map/solve_interpolate/pallas_call | solution.py:836
  168.1 9.4 %reduce_forces.1 = f32[8,128]{1,0:T(8,128)} custom-call(f32[32,8,128]{2,1,0:T(8,128)} %solve_interpolate.1.part_ref), custom_call_target="tpu_custom_call" | custom-call | tf_op jit(solution)/shard_map/reduce_forces/pallas_call | solution.py:880
  177.5 1.3 slice_multiply_fusion
  (26 shorter events, 0.7 us)
Async XLA Ops:
  64.2 0.6 copy-start
  126.4 51.1 %copy-start.1 = (f32[128]{0:T(128)S(1)}, f32[128]{0:T(128)}, u32[]{:S(2)}) copy-start(f32[128]{0:T(128)} %param.16) | copy-start | bytes 1540
